TPU v7x, 32 devices: a 4x4x1 block of a 4x4x8 slice. The times are simulated.
32 devices in a mesh: dp: 1 (over z), sp: 32 (over y, x, core).
Axes of the slice: x: 4, y: 4, z: 1, core: 2. Of those that a mesh axis runs over, the one named last changes fastest.
The devices are a block of a 4x4x8 slice.
Arguments:
- x_patch: bfloat16 [64, 576, 512], P('dp', 'sp')
- w_tok1: bfloat16 [576, 256], P('sp')
- b_tok1: float32 [256], P('sp')
- w_tok2: bfloat16 [256, 576], P(None, 'sp')
- b_tok2: float32 [576], P('sp')
- w_ch1: bfloat16 [512, 2048], replicated
- b_ch1: float32 [2048], replicated
- w_ch2: bfloat16 [2048, 512], replicated
- b_ch2: float32 [512], replicated
- ln1_gain: float32 [512], replicated
- ln1_bias: float32 [512], replicated
- ln2_gain: float32 [512], replicated
- ln2_bias: float32 [512], replicated
Outputs:
- output: bfloat16 [64, 576, 512], P('dp', 'sp')
All inputs are finite; a program needn't handle non-finite values.
Results may differ from a plain program's by a relative error of at most 0.00440373.
Values are sent between devices in bfloat16 or wider.
A program may use at most 768 MiB of HBM per device.

v0:
```python
import jax
import jax.numpy as jnp
from jax import lax
from jax.sharding import PartitionSpec as P

LN_EPS = 1e-6


def layer_norm(values, ln_gain, ln_bias):
    mean_val = jnp.mean(values, axis=-1, keepdims=True)
    centred = values - mean_val
    var_val = jnp.mean(centred * centred, axis=-1, keepdims=True)
    return centred * lax.rsqrt(var_val + LN_EPS) * ln_gain + ln_bias


def channel_mix(x_mid, w_ch1, b_ch1, w_ch2, b_ch2, ln2_gain, ln2_bias):
    mid_wide = x_mid.astype(jnp.float32)
    normed_two = layer_norm(mid_wide, ln2_gain, ln2_bias).astype(jnp.bfloat16)
    ch_pre = jnp.einsum("bsc,cf->bsf", normed_two, w_ch1, preferred_element_type=jnp.float32) + b_ch1
    ch_act = jax.nn.gelu(ch_pre).astype(jnp.bfloat16)
    ch_out = jnp.einsum("bsf,fc->bsc", ch_act, w_ch2, preferred_element_type=jnp.float32) + b_ch2
    return (mid_wide + ch_out).astype(jnp.bfloat16)


def solution(mesh):
    row_spec = P("dp", "sp", None)

    def local_layer(x_blk, w1_rows, b1_part, w2_cols, b2_part, w_ch1, b_ch1, w_ch2, b_ch2, ln1_gain, ln1_bias, ln2_gain, ln2_bias):
        x_wide = x_blk.astype(jnp.float32)
        normed = layer_norm(x_wide, ln1_gain, ln1_bias).astype(jnp.bfloat16)
        part_pre = jnp.einsum("bsc,sd->bdc", normed, w1_rows, preferred_element_type=jnp.float32)
        tok_pre = lax.psum_scatter(part_pre, "sp", scatter_dimension=1, tiled=True) + b1_part[None, :, None]
        tok_act = jax.nn.gelu(tok_pre).astype(jnp.bfloat16)
        act_full = lax.all_gather(tok_act, "sp", axis=1, tiled=True)
        tok_out = jnp.einsum("bdc,ds->bsc", act_full, w2_cols, preferred_element_type=jnp.float32) + b2_part[None, :, None]
        x_mid = (x_wide + tok_out).astype(jnp.bfloat16)
        return channel_mix(x_mid, w_ch1, b_ch1, w_ch2, b_ch2, ln2_gain, ln2_bias)

    in_specs = (row_spec, P("sp", None), P("sp"), P(None, "sp"), P("sp"), P(None, None), P(None), P(None, None), P(None), P(None), P(None), P(None), P(None))
    return jax.shard_map(local_layer, mesh=mesh, in_specs=in_specs, out_specs=row_spec, check_vma=False)
```

profile of v0, /device:TPU:97, one launch (start us, length us, event | category | flops | bytes accessed | tf_op | source)
XLA Modules:
  0.0 332.0 jit_solution(8695864927758693978)
XLA Ops:
  6.5 0.0 copy-start
  6.6 0.0 copy-start.1
  6.6 0.0 reduce-scatter.2.cloned.1.call-start
  6.6 2.2 convert_reduce_fusion.1
  8.8 2.4 fusion.20
  11.2 0.0 copy-done.1
  11.2 15.9 %convolution_bitcast_fusion = f32[64,256,512]{1,2,0:T(8,128)} fusion(bf16[64,18,512]{2,0,1:T(8,128)(2,1)S(1)} %copy-done.1, f32[512]{0:T(512)} %param.23, f32[512]{0:T(512)} %param.22, f32[64,18]{1,0:T(8,128)S(1)} %add_rsqrt_fusion.1, f32[64,18]{1,0:T(8,128)S(1)} %broadcast_multiply_fusion.1, bf16[18,256]{1,0:T(8,128)(2,1)} %param.14), kind=kOutput, calls=%fused_computation.3 | convolution fusion | flops 305528832 | bytes 34756608 | tf_op jit(solution)/shard_map/bsc,sd->bdc/dot_general | solution.py:31
  27.1 34.4 %copy.20 = f32[64,256,512]{2,0,1:T(8,128)} copy(f32[64,256,512]{1,2,0:T(8,128)} %convolution_bitcast_fusion) | data formatting | bytes 67108864 | tf_op jit(solution)/shard_map/bsc,sd->bdc/transpose | solution.py:31
  61.5 0.0 copy-start.6
  61.5 0.0 copy-start.7
  61.5 0.0 copy-start.9
  61.5 0.1 reduce-scatter.2.cloned.1.call-update
  61.6 0.2 all-gather.2.cloned.1.call-start
  61.9 159.9 %reduce-scatter.2.cloned.1.call-done = f32[64,8,512]{2,0,1:T(8,128)} async-done(((f32[64,256,512]{2,0,1:T(8,128)}), f32[64,8,512]{2,0,1:T(8,128)}) %reduce-scatter.2.cloned.1.call-update) | async-done | bytes 1048592 | tf_op jit(solution)/shard_map/reduce_scatter | solution.py:32
  221.7 0.0 copy-done.6
  221.7 2.4 fusion.47
  224.2 0.1 all-gather.2.cloned.1.call-update
  224.2 0.0 copy-start.4
  224.2 0.0 copy-start.5
  224.2 67.9 %all-gather.2.cloned.1.call-done = bf16[64,256,512]{2,0,1:T(8,128)(2,1)} async-done(((bf16[64,8,512]{2,0,1:T(8,128)(2,1)}), bf16[64,256,512]{2,0,1:T(8,128)(2,1)}) %all-gather.2.cloned.1.call-update) | async-done | bytes 16777232 | tf_op jit(solution)/shard_map/all_gather | solution.py:34
  292.2 0.0 copy-done.7
  292.2 0.0 copy-done.9
  292.2 15.6 %convert_reduce_fusion = (f32[64,18]{1,0:T(8,128)S(1)}, bf16[64,18,512]{2,1,0:T(8,128)(2,1)S(1)}) fusion(f32[18]{0:T(128)S(1)} %copy-done.9, bf16[256,18]{0,1:T(8,128)(2,1)S(1)} %copy-done.7, bf16[64,256,512]{2,0,1:T(8,128)(2,1)} %all-gather.2.cloned.1.call-done, bf16[64,18,512]{2,0,1:T(8,128)(2,1)S(1)} %copy-done.1), kind=kOutput, calls=%fused_computation.14 | convolution fusion | flops 305527680 | bytes 19150408 | tf_op jit(solution)/shard_map/bdc,ds->bsc/dot_general | solution.py:35
  307.8 0.0 copy-start.2
  307.8 0.0 copy-start.8
  307.8 0.8 fusion.16
  308.6 0.3 copy-done.2
  308.9 0.0 copy-done.4
  308.9 0.0 copy-done.5
  308.9 2.0 fusion.19
  311.0 0.0 copy-done
  311.0 0.0 copy-done.8
  311.0 0.0 copy-start.3
  311.0 9.2 %fusion.10 = f32[64,18,512]{2,0,1:T(8,128)} fusion(f32[2048]{0:T(1024)S(1)} %copy-done.8, bf16[2048,512]{1,0:T(8,128)(2,1)S(1)} %copy-done, bf16[512,2048]{1,0:T(8,128)(2,1)} %param.18, bf16[64,18,512]{2,1,0:T(8,128)(2,1)} %fusion.19), kind=kOutput, calls=%fused_computation.18 | convolution fusion | flops 4855431168 | bytes 7741440 | tf_op jit(solution)/shard_map/bsf,fc->bsc/dot_general | solution.py:21
  320.2 0.0 copy-done.3
  320.2 3.5 %fusion.25 = bf16[64,18,512]{2,1,0:T(8,128)(2,1)S(1)} fusion(bf16[64,18,512]{2,1,0:T(8,128)(2,1)} %copy-done.2, f32[64,18,512]{2,0,1:T(8,128)} %fusion.10, f32[512]{0:T(512)S(1)} %copy-done.3), kind=kLoop, calls=%fused_computation.32 | loop fusion | flops 2359296 | bytes 4720640 | tf_op jit(solution)/shard_map/convert_element_type | solution.py:22
  323.7 1.4 copy.24
  (4 shorter events, 0.0 us)
Async XLA Ops:
  6.5 304.4 %copy-start = (bf16[2048,512]{1,0:T(8,128)(2,1)S(1)}, bf16[2048,512]{1,0:T(8,128)(2,1)}, u32[]{:S(2)}) copy-start(bf16[2048,512]{1,0:T(8,128)(2,1)} %param.20) | copy-start | bytes 6291460
  6.6 4.6 %copy-start.1 = (bf16[64,18,512]{2,0,1:T(8,128)(2,1)S(1)}, bf16[64,18,512]{2,0,1:T(8,128)(2,1)}, u32[]{:S(2)}) copy-start(bf16[64,18,512]{2,0,1:T(8,128)(2,1)} %param.13) | copy-start | bytes 3538948
  6.6 215.2 %reduce-scatter.2.cloned.1.call-start = ((), (), s32[]{:S(2)}) async-start(), calls=%async_computation.1 | async-start | bytes 34603008 | tf_op jit(solution)/shard_map/reduce_scatter | solution.py:32
  61.5 160.2 %copy-start.6 = (f32[8]{0:T(128)S(1)}, f32[8]{0:T(128)}, u32[]{:S(2)}) copy-start(f32[8]{0:T(128)} %param.15) | copy-start | bytes 100
  61.5 230.6 %copy-start.7 = (bf16[256,18]{0,1:T(8,128)(2,1)S(1)}, bf16[256,18]{0,1:T(8,128)(2,1)}, u32[]{:S(2)}) copy-start(bf16[256,18]{0,1:T(8,128)(2,1)} %param.16) | copy-start | bytes 27652
  61.5 230.6 %copy-start.9 = (f32[18]{0:T(128)S(1)}, f32[18]{0:T(128)}, u32[]{:S(2)}) copy-start(f32[18]{0:T(128)} %param.17) | copy-start | bytes 220
  61.6 230.6 %all-gather.2.cloned.1.call-start = ((), (), s32[]{:S(2)}) async-start(), calls=%async_computation.2 | async-start | bytes 17301504 | tf_op jit(solution)/shard_map/all_gather | solution.py:34
  224.2 84.7 %copy-start.4 = (f32[512]{0:T(512)S(1)}, f32[512]{0:T(512)}, u32[]{:S(2)}) copy-start(f32[512]{0:T(512)} %param.25) | copy-start | bytes 6148
  224.2 84.7 %copy-start.5 = (f32[512]{0:T(512)S(1)}, f32[512]{0:T(512)}, u32[]{:S(2)}) copy-start(f32[512]{0:T(512)} %param.24) | copy-start | bytes 6148
  307.8 1.2 copy-start.2
  307.8 3.2 copy-start.8
  311.0 9.2 %copy-start.3 = (f32[512]{0:T(512)S(1)}, f32[512]{0:T(512)}, u32[]{:S(2)}) copy-start(f32[512]{0:T(512)} %param.21) | copy-start | bytes 6148
Sparse Core Ops, SparseCore 0:
  61.7 159.9 reduce-scatter.1
  224.3 67.7 all-gather.1
where the time goes:
time: 333 us; the launch traced here: 332 us
  waiting for transfers between devices  228 us (68%)
  matrix products  40.7 us (12%)
  local copies, waits for them, and re-layouts  36.1 us (11%)
  between operations  13.5 us (4%)
  other arithmetic  13.4 us (4%)
    reduce_scatter x1, waiting for transfers between devices, local_layer(): lax.psum_scatter(part_pre, 'sp', scatter_dimension=1, tiled=True)  160 us
    all_gather x1, waiting for transfers between devices, local_layer(): act_full = lax.all_gather(tok_act, 'sp', axis=1, tiled=True)  67.9 us
    transpose x1, local copies, waits for them, and re-layouts, local_layer(): jnp.einsum('bsc,sd->bdc', normed, w1_rows, preferred_element_type=jnp.flo...  34.4 us
    dot_general x1, matrix products, local_layer(): jnp.einsum('bsc,sd->bdc', normed, w1_rows, preferred_element_type=jnp.flo...  15.9 us
    dot_general x1, matrix products, local_layer(): jnp.einsum('bdc,ds->bsc', act_full, w2_cols, preferred_element_type=jnp.f...  15.6 us
    dot_general x1, matrix products, channel_mix(): jnp.einsum('bsf,fc->bsc', ch_act, w_ch2, preferred_element_type=jnp.float32)  9.23 us
  transfers between devices with their start and end apart: 2, of which 2 were waited for; matrix products, arithmetic and copies ran while one was open for 0% of the time, Pallas kernels for 0%

commit v1 on v0

--- a/solution.py
+++ b/solution.py
@@ -26,15 +26,19 @@
     row_spec = P("dp", "sp", None)
 
     def local_layer(x_blk, w1_rows, b1_part, w2_cols, b2_part, w_ch1, b_ch1, w_ch2, b_ch2, ln1_gain, ln1_bias, ln2_gain, ln2_bias):
-        x_wide = x_blk.astype(jnp.float32)
+        x_img = lax.all_to_all(x_blk, "sp", split_axis=0, concat_axis=1, tiled=True)
+        w1 = lax.all_gather(w1_rows, "sp", axis=0, tiled=True)
+        w2 = lax.all_gather(w2_cols, "sp", axis=1, tiled=True)
+        b1 = lax.all_gather(b1_part, "sp", axis=0, tiled=True)
+        b2 = lax.all_gather(b2_part, "sp", axis=0, tiled=True)
+        x_wide = x_img.astype(jnp.float32)
         normed = layer_norm(x_wide, ln1_gain, ln1_bias).astype(jnp.bfloat16)
-        part_pre = jnp.einsum("bsc,sd->bdc", normed, w1_rows, preferred_element_type=jnp.float32)
-        tok_pre = lax.psum_scatter(part_pre, "sp", scatter_dimension=1, tiled=True) + b1_part[None, :, None]
+        tok_pre = jnp.einsum("sd,bsc->bdc", w1, normed, preferred_element_type=jnp.float32) + b1[None, :, None]
         tok_act = jax.nn.gelu(tok_pre).astype(jnp.bfloat16)
-        act_full = lax.all_gather(tok_act, "sp", axis=1, tiled=True)
-        tok_out = jnp.einsum("bdc,ds->bsc", act_full, w2_cols, preferred_element_type=jnp.float32) + b2_part[None, :, None]
+        tok_out = jnp.einsum("ds,bdc->bsc", w2, tok_act, preferred_element_type=jnp.float32) + b2[None, :, None]
         x_mid = (x_wide + tok_out).astype(jnp.bfloat16)
-        return channel_mix(x_mid, w_ch1, b_ch1, w_ch2, b_ch2, ln2_gain, ln2_bias)
+        z_img = channel_mix(x_mid, w_ch1, b_ch1, w_ch2, b_ch2, ln2_gain, ln2_bias)
+        return lax.all_to_all(z_img, "sp", split_axis=1, concat_axis=0, tiled=True)
 
     in_specs = (row_spec, P("sp", None), P("sp"), P(None, "sp"), P("sp"), P(None, None), P(None), P(None, None), P(None), P(None), P(None), P(None), P(None))
     return jax.shard_map(local_layer, mesh=mesh, in_specs=in_specs, out_specs=row_spec, check_vma=False)

time: 333 us -> 193 us (0.58)
  waiting for transfers between devices: 228 us -> 0.01 us
  blocking collectives: 0 us -> 147 us
  matrix products: 40.7 us -> 12.7 us
  local copies, waits for them, and re-layouts: 36.1 us -> 10.4 us
  between operations: 13.5 us -> 0.17 us
  starting transfers between devices: 0.25 us -> 9.14 us
    reduce_scatter x1 -> x0, waiting for transfers between devices: 160 us -> none  [local_layer(): lax.psum_scatter(part_pre, 'sp', scatter_dimension=1, tiled=True)]
    all_gather x0 -> x2, blocking collectives: none -> 76.1 us  [the longest x1 43 us: local_layer(): w1 = lax.all_gather(w1_rows, 'sp', axis=0, tiled=True)]
    all_gather x1 -> x0, waiting for transfers between devices: 67.9 us -> none  [local_layer(): act_full = lax.all_gather(tok_act, 'sp', axis=1, tiled=True)]
    unnamed x0 -> x1, blocking collectives: none -> 49.1 us
    transpose x1 -> x0, local copies, waits for them, and re-layouts: 34.4 us -> none  [local_layer(): jnp.einsum('bsc,sd->bdc', normed, w1_rows, preferred_element_type=jnp.flo...]
    dot_general x2 -> x1, matrix products: 31.5 us -> 4.56 us  [local_layer(): jnp.einsum('ds,bdc->bsc', w2, tok_act, preferred_element_type=jnp.float32)]
    all_to_all x0 -> x1, blocking collectives: none -> 22.3 us  [local_layer(): return lax.all_to_all(z_img, 'sp', split_axis=1, concat_axis=0, tiled=True)]
    all_to_all x0 -> x1, starting transfers between devices: none -> 9.14 us  [local_layer(): x_img = lax.all_to_all(x_blk, 'sp', split_axis=0, concat_axis=1, tiled=True)]
  transfers between devices with their start and end apart: 2 -> 1, of which waited for: 2 -> 0; matrix products, arithmetic and copies ran while one was open for 0% -> 1% of each run, Pallas kernels for 0% -> 0%
where the time goes in v1:
time: 193 us
  blocking collectives  147 us (76%)
  other arithmetic  12.8 us (7%)
  matrix products  12.7 us (7%)
  local copies, waits for them, and re-layouts  10.4 us (5%)
  starting transfers between devices  9.14 us (5%)
    unnamed x1, blocking collectives  49.1 us
    all_gather x1, blocking collectives, local_layer(): w1 = lax.all_gather(w1_rows, 'sp', axis=0, tiled=True)  43 us
    all_gather x1, blocking collectives, local_layer(): w2 = lax.all_gather(w2_cols, 'sp', axis=1, tiled=True)  33.1 us
    all_to_all x1, blocking collectives, local_layer(): return lax.all_to_all(z_img, 'sp', split_axis=1, concat_axis=0, tiled=True)  22.3 us
    all_to_all x1, starting transfers between devices, local_layer(): x_img = lax.all_to_all(x_blk, 'sp', split_axis=0, concat_axis=1, tiled=True)  9.14 us
    dot_general x1, matrix products, channel_mix(): jnp.einsum('bsf,fc->bsc', ch_act, w_ch2, preferred_element_type=jnp.float32)  8.15 us
    unnamed x29, local copies, waits for them, and re-layouts  5.33 us
    reduce_sum x2, other arithmetic, layer_norm(): var_val = jnp.mean(centred * centred, axis=-1, keepdims=True)  4.81 us
  transfers between devices with their start and end apart: 1, of which 0 were waited for; matrix products, arithmetic and copies ran while one was open for 1% of the time, Pallas kernels for 0%

profile of v1, /device:TPU:97, one launch (start us, length us, event | category | flops | bytes accessed | tf_op | source)
XLA Modules:
  0.0 192.7 jit_solution(6296084765064729253)
XLA Ops:
  0.0 0.0 copy-start
  0.0 0.0 copy-start.1
  0.0 3.3 %copy.45 = bf16[64,18,512]{2,1,0:T(8,128)(2,1)} copy(bf16[64,18,512]{2,0,1:T(8,128)(2,1)} %param.13) | data formatting | bytes 2359296 | tf_op args[0]
  3.3 0.0 copy-start.2
  3.3 0.0 copy-start.9
  3.3 0.0 copy-start.10
  3.3 9.1 %all-to-all-start = ((bf16[64,18,512]{2,1,0:T(8,128)(2,1)}), bf16[64,18,512]{2,1,0:T(8,128)(2,1)}, u32[]{:S(2)}, u32[]{:S(2)}) async-start(bf16[64,18,512]{2,1,0:T(8,128)(2,1)} %copy.45), calls=%async_computation | async-start | bytes 3145728 | tf_op jit(solution)/shard_map/all_to_all | solution.py:29
  12.4 0.0 copy-done.1
  12.4 43.0 %all-gather = bf16[32,18,256]{2,1,0:T(8,128)(2,1)S(1)} all-gather(bf16[1,18,256]{2,1,0:T(8,128)(2,1)S(1)} %bitcast.52), channel_id=1, replica_groups=mesh['dp'=1,'sp'=32] {'sp'}, dimensions={0}, use_global_device_ids=true | all-gather | bytes 304128 | tf_op jit(solution)/shard_map/all_gather | solution.py:30
  55.4 0.8 reshape.66
  56.2 0.0 copy-done.2
  56.2 33.1 %all-gather.1 = bf16[32,18,256]{2,1,0:T(8,128)(2,1)S(1)} all-gather(bf16[1,18,256]{2,1,0:T(8,128)(2,1)S(1)} %bitcast.53), channel_id=1, replica_groups=mesh['dp'=1,'sp'=32] {'sp'}, dimensions={0}, use_global_device_ids=true | all-gather | bytes 304128 | tf_op jit(solution)/shard_map/all_gather | solution.py:31
  89.3 0.8 reshape.67
  90.1 0.0 copy-done.9
  90.1 0.2 dynamic-update-slice
  90.3 0.0 copy-done.10
  90.3 0.2 dynamic-update-slice.1
  90.6 49.1 %all-reduce.2 = (f32[576]{0:T(1024)S(1)}, f32[256]{0:T(256)S(1)}) all-reduce(f32[576]{0:T(1024)S(1)} %dynamic-update-slice.1, f32[256]{0:T(256)S(1)} %dynamic-update-slice), channel_id=1, replica_groups=mesh['dp'=1,'sp'=32] {'sp'}, use_global_device_ids=true, to_apply=%add.1 | all-reduce | flops 832 | bytes 6656
  139.6 0.0 all-to-all-done
  139.6 3.9 %bitcast_reduce_fusion = (f32[2,32,18]{0,2,1:T(8,128)S(1)}, f32[32,2,18,512]{3,1,2,0:T(2,128)}) fusion(bf16[32,2,18,512]{3,2,1,0:T(8,128)(2,1)} %bitcast.13), kind=kLoop, calls=%fused_computation.22 | loop fusion | flops 588672 | bytes 3543552 | tf_op jit(solution)/shard_map/reduce_sum | solution.py:10
  143.6 0.7 reshape.73
  144.3 0.0 copy-start.3
  144.3 0.0 copy-start.4
  144.3 3.0 %fusion.19 = f32[2,32,18]{0,2,1:T(8,128)S(1)} fusion(f32[32,2,18,512]{3,1,2,0:T(2,128)} %get-tuple-element.8, f32[2,32,18]{0,2,1:T(8,128)S(1)} %broadcast_multiply_fusion), kind=kLoop, calls=%fused_computation.25 | loop fusion | flops 1768320 | bytes 2368512 | tf_op jit(solution)/shard_map/reduce_sum | solution.py:12
  147.3 0.1 add_rsqrt_fusion
  147.4 0.7 reshape.72
  148.2 0.0 copy-done.3
  148.2 0.0 copy-done.4
  148.2 4.0 %add_convert_fusion = bf16[2,576,512]{2,0,1:T(2,128)(2,1)S(1)} fusion(f32[512]{0:T(512)S(1)} %copy-done.3, f32[512]{0:T(512)S(1)} %copy-done.4, f32[2,576]{0,1:T(8,128)} %reshape.72, f32[2,576]{0,1:T(8,128)} %reshape.73, f32[32,2,18,512]{3,1,2,0:T(2,128)} %get-tuple-element.8), kind=kLoop, calls=%fused_computation.26 | loop fusion | flops 2949120 | bytes 3552256 | tf_op jit(solution)/shard_map/convert_element_type | solution.py:35
  152.1 0.0 copy-start.5
  152.1 0.0 copy-start.6
  152.1 0.0 copy-start.7
  152.2 0.0 copy-start.8
  152.2 4.6 %convert_reduce_fusion = (f32[2,576]{1,0:T(2,128)S(1)}, bf16[2,576,512]{2,1,0:T(8,128)(2,1)}) fusion(f32[576]{0:T(1024)S(1)} %get-tuple-element.5, bf16[576,256,1]{1,0,2:T(8,128)(2,1)} %reshape.67, bf16[576,256,1]{1,0,2:T(8,128)(2,1)} %reshape.66, bf16[2,576,512]{2,0,1:T(2,128)(2,1)S(1)} %add_convert_fusion, f32[256]{0:T(256)S(1)} %get-tuple-element.6, ...), kind=kOutput, calls=%fused_computation.12 | convolution fusion | flops 609549184 | bytes 5316352 | tf_op jit(solution)/shard_map/ds,bdc->bsc/dot_general | solution.py:38
  156.7 1.8 fusion.12
  158.5 0.0 copy-done
  158.6 0.0 copy-done.5
  158.6 0.0 copy-done.6
  158.6 0.0 copy-done.7
  158.6 0.0 copy-done.8
  158.6 8.1 %fusion.16 = bf16[2,576,512]{2,1,0:T(8,128)(2,1)S(1)} fusion(bf16[2,576,512]{2,1,0:T(8,128)(2,1)} %get-tuple-element.10, bf16[2048,512]{1,0:T(8,128)(2,1)S(1)} %copy-done, f32[2048]{0:T(1024)S(1)} %copy-done.5, bf16[512,2048]{1,0:T(8,128)(2,1)} %param.18, f32[512]{0:T(512)S(1)} %copy-done.6, f32[512]{0:T(512)S(1)} %copy-done.7, f32[512]{0:T(512)S(1)} %copy-done.8, ...), kind=kOutput, calls=%fused_computation.19 | convolution fusion | flops 4861329408 | bytes 6577152 | tf_op jit(solution)/shard_map/bsf,fc->bsc/dot_general | solution.py:21
  166.8 1.2 copy.57
  168.0 22.3 %all_to_all.27 = bf16[2,576,512]{2,0,1:T(2,128)(2,1)S(1)} all-to-all(bf16[2,576,512]{2,0,1:T(2,128)(2,1)S(1)} %copy.57), channel_id=1, replica_groups=mesh['dp'=1,'sp'=32] {'sp'}, dimensions={1} | all-to-all | bytes 2359296 | tf_op jit(solution)/shard_map/all_to_all | solution.py:41
  190.3 1.1 copy.58
  191.4 1.3 all_to_all.24
  (5 shorter events, 0.0 us)
Async XLA Ops:
  0.0 158.5 %copy-start = (bf16[2048,512]{1,0:T(8,128)(2,1)S(1)}, bf16[2048,512]{1,0:T(8,128)(2,1)}, u32[]{:S(2)}) copy-start(bf16[2048,512]{1,0:T(8,128)(2,1)} %param.20) | copy-start | bytes 6291460
  0.0 12.4 %copy-start.1 = (bf16[18,256]{1,0:T(8,128)(2,1)S(1)}, bf16[18,256]{1,0:T(8,128)(2,1)}, u32[]{:S(2)}) copy-start(bf16[18,256]{1,0:T(8,128)(2,1)} %param.14) | copy-start | bytes 27652
  3.3 52.9 %copy-start.2 = (bf16[256,18]{0,1:T(8,128)(2,1)S(1)}, bf16[256,18]{0,1:T(8,128)(2,1)}, u32[]{:S(2)}) copy-start(bf16[256,18]{0,1:T(8,128)(2,1)} %param.16) | copy-start | bytes 27652
  3.3 86.9 %copy-start.9 = (f32[8]{0:T(128)S(1)}, f32[8]{0:T(128)}, u32[]{:S(2)}) copy-start(f32[8]{0:T(128)} %param.15) | copy-start | bytes 100
  3.3 87.1 %copy-start.10 = (f32[18]{0:T(128)S(1)}, f32[18]{0:T(128)}, u32[]{:S(2)}) copy-start(f32[18]{0:T(128)} %param.17) | copy-start | bytes 220
  3.3 136.4 %all-to-all-start = ((bf16[64,18,512]{2,1,0:T(8,128)(2,1)}), bf16[64,18,512]{2,1,0:T(8,128)(2,1)}, u32[]{:S(2)}, u32[]{:S(2)}) async-start(bf16[64,18,512]{2,1,0:T(8,128)(2,1)} %copy.45), calls=%async_computation | async-start | bytes 3145728 | tf_op jit(solution)/shard_map/all_to_all | solution.py:29
  144.3 3.8 %copy-start.3 = (f32[512]{0:T(512)S(1)}, f32[512]{0:T(512)}, u32[]{:S(2)}) copy-start(f32[512]{0:T(512)} %param.23) | copy-start | bytes 6148
  144.3 3.8 %copy-start.4 = (f32[512]{0:T(512)S(1)}, f32[512]{0:T(512)}, u32[]{:S(2)}) copy-start(f32[512]{0:T(512)} %param.22) | copy-start | bytes 6148
  152.1 6.4 %copy-start.5 = (f32[2048]{0:T(1024)S(1)}, f32[2048]{0:T(1024)}, u32[]{:S(2)}) copy-start(f32[2048]{0:T(1024)} %param.19) | copy-start | bytes 24580
  152.1 6.4 %copy-start.6 = (f32[512]{0:T(512)S(1)}, f32[512]{0:T(512)}, u32[]{:S(2)}) copy-start(f32[512]{0:T(512)} %param.21) | copy-start | bytes 6148
  152.1 6.4 %copy-start.7 = (f32[512]{0:T(512)S(1)}, f32[512]{0:T(512)}, u32[]{:S(2)}) copy-start(f32[512]{0:T(512)} %param.25) | copy-start | bytes 6148
  152.2 6.4 %copy-start.8 = (f32[512]{0:T(512)S(1)}, f32[512]{0:T(512)}, u32[]{:S(2)}) copy-start(f32[512]{0:T(512)} %param.24) | copy-start | bytes 6148

commit v2 on v0

v2 whole, which is shorter than its diff:
```python
import functools
import math

import jax
import jax.numpy as jnp
from jax import lax
from jax.experimental import pallas as pl
from jax.experimental.pallas import tpu as pltpu
from jax.sharding import PartitionSpec as P

LN_EPS = 1e-6
AXIS = "sp"
LANES = 128
CORES = 2
VMEM_LIMIT = 67043328
BF16 = jnp.bfloat16
F32 = jnp.float32


def layer_norm(values, ln_gain, ln_bias):
    mean_val = jnp.mean(values, axis=-1, keepdims=True)
    centred = values - mean_val
    var_val = jnp.mean(centred * centred, axis=-1, keepdims=True)
    return centred * lax.rsqrt(var_val + LN_EPS) * ln_gain + ln_bias


def gelu(a):
    return 0.5 * a * (1.0 + jnp.tanh(math.sqrt(2.0 / math.pi) * (a + 0.044715 * (a * a * a))))


def widen(column, copies):
    return jnp.concatenate([column] * copies, axis=1)


def mixer_kernel(
    n, chunks, ff_tile,
    x_hbm, w1_hbm, w2_hbm, b1_ref, b2_ref, wc1_hbm, bc1_ref, wc2_hbm, bc2_ref, g1_ref, o1_ref, g2_ref, o2_ref,
    out_ref,
    x_own, x_img, z_img, w_own, w_all, w1_t, w2_big, b_own, b_all, b1_col, b2_col, h_acc, act, wc1, wc2, tally, w_tally, b_tally,
    local_sem, mine_sem, own_sem, chan_sem, w_send, w_recv, d_send, d_recv, b_send, b_recv, x_send, x_recv, z_send, z_recv,
):
    me = lax.axis_index(AXIS)
    side = math.isqrt(n // CORES)
    my_core = lax.rem(me, CORES)
    my_x = lax.rem(me // CORES, side)
    my_y = me // (CORES * side)
    patches, rows, chans = x_img.shape
    pairs = patches // 2
    hid = w1_hbm.shape[1]
    per = patches // chunks
    m = per * rows

    def peer(k):
        core = lax.rem(my_core + lax.rem(k, CORES), CORES)
        col = lax.rem(my_x + lax.rem(k // CORES, side), side)
        row = lax.rem(my_y + k // (CORES * side), side)
        return (row * side + col) * CORES + core

    def two(j):
        return pl.ds(pl.multiple_of(2 * j, 2), 2)

    def settle(counted, sem):
        pltpu.make_async_copy(counted, counted, sem).wait()

    loads = [pltpu.make_async_copy(x_hbm, x_own, local_sem.at[0])]
    for q in range(pairs):
        loads.append(pltpu.make_async_copy(w1_hbm.at[pl.ds(2 * q, 2), :], w_own.at[q, :, pl.ds(0, hid)], local_sem.at[1 + q]))
        loads.append(pltpu.make_async_copy(w2_hbm.at[pl.ds(2 * q, 2), :], w_own.at[q, :, pl.ds(hid, hid)], local_sem.at[1 + pairs + q]))
    mine = [pltpu.make_async_copy(x_hbm.at[:, two(me), :], x_img.at[:, two(me), :], mine_sem.at[0])]
    for q in range(pairs):
        mine.append(pltpu.make_async_copy(w1_hbm.at[pl.ds(2 * q, 2), :], w_all.at[q, two(me), pl.ds(0, hid)], mine_sem.at[1 + q]))
        mine.append(pltpu.make_async_copy(w2_hbm.at[pl.ds(2 * q, 2), :], w_all.at[q, two(me), pl.ds(hid, hid)], mine_sem.at[1 + pairs + q]))
    for c in loads + mine:
        c.start()
    chan_loads = [pltpu.make_async_copy(wc1_hbm, wc1, chan_sem.at[0]), pltpu.make_async_copy(wc2_hbm, wc2, chan_sem.at[1])]
    for c in chan_loads:
        c.start()
    b_own[...] = jnp.zeros_like(b_own)
    is_mine = lax.broadcasted_iota(jnp.int32, (rows, LANES), 0) // 2 == me
    for i, b_ref in enumerate((b1_ref, b2_ref)):
        b_own[i, :, pl.ds(0, b_ref.shape[1])] = jnp.broadcast_to(b_ref[...], (2, b_ref.shape[1]))
        b_all[i] = jnp.where(is_mine, jnp.broadcast_to(b_own[i, pl.ds(0, 1), :], (rows, LANES)), 0.0)

    barrier = pltpu.get_barrier_semaphore()

    @pl.loop(0, n)
    def _(k):
        pl.semaphore_signal(barrier, inc=1, device_id={AXIS: peer(k)})

    pl.semaphore_wait(barrier, n)
    for c in loads + mine:
        c.wait()

    def remote(src, dst, ss, rs, j):
        return pltpu.make_async_remote_copy(src_ref=src, dst_ref=dst, send_sem=ss, recv_sem=rs, device_id={AXIS: j})

    @pl.loop(1, n // CORES)
    def _(k):
        remote(w_own, w_all.at[:, two(me), :], w_send, w_recv, peer(CORES * k)).start()

    @pl.loop(1, n)
    def _(k):
        remote(b_own, b_all.at[:, two(me), :], b_send, b_recv, peer(k)).start()

    for t in range(chunks):
        part = pl.ds(t * per, per)

        @pl.loop(1, n)
        def _(k):
            j = peer(k)
            remote(x_own.at[part, two(j), :], x_img.at[part, two(me), :], x_send, x_recv.at[t], j).start()

    half = w_all.at[:, pl.ds(0, n), :]
    settle(w_tally, w_recv)
    other = peer(1)

    @pl.loop(0, n // CORES)
    def _(k):
        blk = w_all.at[:, two(CORES * k + my_core), :]
        remote(blk, blk, d_send, d_recv, other).start()

    settle(half, d_recv)
    settle(b_tally, b_recv)

    even = lax.rem(lax.broadcasted_iota(jnp.int32, (rows, 2 * hid), 0), 2) == 0
    keep = even == (lax.broadcasted_iota(jnp.int32, (rows, 2 * hid), 1) < hid)
    for q in range(pairs):
        wq = w_all[q].astype(F32)
        first = jnp.where(even, wq, pltpu.roll(wq, 1, 0))
        second = jnp.where(even, pltpu.roll(wq, rows - 1, 0), wq)
        ones, twos = [], []
        for d in (first, second):
            ones.append(jnp.where(keep, jnp.concatenate([d[:, :hid]] * 2, axis=1), 0.0))
            twos.append(jnp.where(keep, jnp.concatenate([d[:, hid:]] * 2, axis=1), 0.0))
        w1_t[:, pl.ds(2 * rows * q, 2 * rows)] = jnp.transpose(jnp.concatenate(ones, axis=0)).astype(BF16)
        w2_big[pl.ds(2 * rows * q, 2 * rows), :] = jnp.concatenate(twos, axis=0).astype(BF16)

    per_dev = hid // n
    picked = b_all[0, pl.ds(0, n, stride=2), :]
    spread = jnp.broadcast_to(picked.reshape(n, 1, LANES), (n, per_dev, LANES))
    diag = lax.broadcasted_iota(jnp.int32, spread.shape, 1) == lax.broadcasted_iota(jnp.int32, spread.shape, 2)
    col1 = jnp.broadcast_to(jnp.sum(jnp.where(diag, spread, 0.0), axis=2, keepdims=True), spread.shape)
    for i in range(2):
        b1_col[pl.ds(hid * i, hid), :] = col1.reshape(hid, LANES)
    tail = b_all[1]
    for s in range(patches):
        b2_col[pl.ds(rows * s, rows), :] = jnp.broadcast_to(tail[:, s : s + 1], (rows, LANES))

    wide = chans // LANES
    for t in range(chunks):
        part = x_img.at[pl.ds(t * per, per)]
        settle(tally.at[:, pl.ds(0, per)], x_recv.at[t])
        u = layer_norm(part[...].reshape(m, chans).astype(F32), g1_ref[...], o1_ref[...]).astype(BF16)
        term = jnp.dot(w1_t[:, pl.ds(t * m, m)], u, preferred_element_type=F32)
        h_acc[...] = term if t == 0 else h_acc[...] + term
    g = gelu(h_acc[...] + widen(b1_col[...], wide)).astype(BF16)
    for c in chan_loads:
        c.wait()

    ff = wc1.shape[1]
    owns = []
    for t in range(chunks):
        part = pl.ds(t * per, per)
        tok = jnp.dot(w2_big[pl.ds(t * m, m), :], g, preferred_element_type=F32) + widen(b2_col[pl.ds(t * m, m), :], wide)
        x_mid = (x_img[part].reshape(m, chans).astype(F32) + tok).astype(BF16)
        mid_wide = x_mid.astype(F32)
        v = layer_norm(mid_wide, g2_ref[...], o2_ref[...]).astype(BF16)
        for f in range(ff // ff_tile):
            cols = pl.ds(f * ff_tile, ff_tile)
            pre = jnp.dot(v, wc1[:, cols], preferred_element_type=F32) + bc1_ref[:, cols]
            act[:, cols] = gelu(pre).astype(BF16)
        ch_out = jnp.dot(act[...], wc2[...], preferred_element_type=F32) + bc2_ref[...]
        z_img[part] = (mid_wide + ch_out).astype(BF16).reshape(per, rows, chans)

        own = pltpu.make_async_copy(z_img.at[part, two(me), :], out_ref.at[part, two(me), :], own_sem.at[t])
        own.start()
        owns.append(own)

        @pl.loop(1, n)
        def _(k):
            j = peer(k)
            remote(z_img.at[part, two(j), :], out_ref.at[part, two(me), :], z_send, z_recv, j).start()

    for c in owns:
        c.wait()
    for counted, sem in ((tally, z_recv), (tally, z_send), (tally, x_send), (w_tally, w_send), (b_tally, b_send), (half, d_send)):
        settle(counted, sem)


def solution(mesh, chunks=3, ff_tile=512):
    row_spec = P("dp", AXIS, None)
    n = mesh.shape[AXIS]

    def local_layer(x_blk, w1_rows, b1_part, w2_cols, b2_part, w_ch1, b_ch1, w_ch2, b_ch2, ln1_gain, ln1_bias, ln2_gain, ln2_bias):
        x_t = jnp.transpose(x_blk, (1, 0, 2))
        w2_rows = jnp.transpose(w2_cols)
        patches, rows, chans = x_t.shape
        hid = w1_rows.shape[1]
        ff = w_ch1.shape[1]
        m = patches // chunks * rows
        any_spec = pl.BlockSpec(memory_space=pltpu.HBM)
        vm = pl.BlockSpec(memory_space=pltpu.VMEM)
        sem = pltpu.SemaphoreType.DMA
        z_t = pl.pallas_call(
            functools.partial(mixer_kernel, n, chunks, ff_tile),
            name="mixer",
            out_shape=jax.ShapeDtypeStruct(x_t.shape, BF16),
            in_specs=[any_spec, any_spec, any_spec, vm, vm, any_spec, vm, any_spec, vm, vm, vm, vm, vm],
            out_specs=any_spec,
            scratch_shapes=[
                pltpu.VMEM(x_t.shape, BF16),
                pltpu.VMEM(x_t.shape, BF16),
                pltpu.VMEM(x_t.shape, BF16),
                pltpu.VMEM((patches // 2, 2, 2 * hid), BF16),
                pltpu.VMEM((patches // 2, rows, 2 * hid), BF16),
                pltpu.VMEM((2 * hid, patches * rows), BF16),
                pltpu.VMEM((patches * rows, 2 * hid), BF16),
                pltpu.VMEM((2, 2, LANES), F32),
                pltpu.VMEM((2, rows, LANES), F32),
                pltpu.VMEM((2 * hid, LANES), F32),
                pltpu.VMEM((patches * rows, LANES), F32),
                pltpu.VMEM((2 * hid, chans), F32),
                pltpu.VMEM((m, ff), BF16),
                pltpu.VMEM(w_ch1.shape, BF16),
                pltpu.VMEM(w_ch2.shape, BF16),
                pltpu.VMEM((n - 1, patches, 2, chans), BF16),
                pltpu.VMEM((n // CORES - 1, patches // 2, 2, 2 * hid), BF16),
                pltpu.VMEM((n - 1, 2, 2, LANES), F32),
                sem((1 + patches,)),
                sem((1 + patches,)),
                sem((chunks,)),
                sem((2,)),
                sem, sem, sem, sem, sem, sem, sem,
                sem((chunks,)),
                sem, sem,
            ],
            compiler_params=pltpu.CompilerParams(collective_id=0, has_side_effects=True, vmem_limit_bytes=VMEM_LIMIT),
        )(
            x_t, w1_rows, w2_rows, b1_part[None, :], b2_part[None, :], w_ch1, b_ch1[None, :], w_ch2, b_ch2[None, :],
            ln1_gain[None, :], ln1_bias[None, :], ln2_gain[None, :], ln2_bias[None, :],
        )
        return jnp.transpose(z_t, (1, 0, 2))

    in_specs = (row_spec, P(AXIS, None), P(AXIS), P(None, AXIS), P(AXIS), P(None, None), P(None), P(None, None), P(None), P(None), P(None), P(None), P(None))
    return jax.shard_map(local_layer, mesh=mesh, in_specs=in_specs, out_specs=row_spec, check_vma=False)
```

time: 333 us -> 54.2 us (0.16)
  waiting for transfers between devices: 228 us -> 0 us
  Pallas kernels: 0 us -> 51.7 us
  matrix products: 40.7 us -> 0 us
  local copies, waits for them, and re-layouts: 36.1 us -> 2.39 us
  between operations: 13.5 us -> 0.01 us
  other arithmetic: 13.4 us -> 0 us
    reduce_scatter x1 -> x0, waiting for transfers between devices: 160 us -> none  [local_layer(): lax.psum_scatter(part_pre, 'sp', scatter_dimension=1, tiled=True)]
    all_gather x1 -> x0, waiting for transfers between devices: 67.9 us -> none  [local_layer(): act_full = lax.all_gather(tok_act, 'sp', axis=1, tiled=True)]
    pallas_call x0 -> x1, Pallas kernels: none -> 51.7 us  [local_layer(): pl.pallas_call(functools.partial(mixer_kernel, n, chunks, ff_tile), name=...]
    dot_general x3 -> x0, matrix products: 40.7 us -> none  [the longest x1 15.9 us: local_layer(): jnp.einsum('bsc,sd->bdc', normed, w1_rows, preferred_element_type=jnp.flo...]
    transpose x1 -> x0, local copies, waits for them, and re-layouts: 34.4 us -> none  [local_layer(): jnp.einsum('bsc,sd->bdc', normed, w1_rows, preferred_element_type=jnp.flo...]
    convert_element_type x3 -> x0, other arithmetic: 8 us -> none  [the longest x1 3.53 us: channel_mix(): return (mid_wide + ch_out).astype(jnp.bfloat16)]
    reduce_sum x3 -> x0, other arithmetic: 5.36 us -> none  [the longest x2 3.18 us: layer_norm(): var_val = jnp.mean(centred * centred, axis=-1, keepdims=True)]
  transfers between devices with their start and end apart: 2 -> 0, of which waited for: 2 -> 0; matrix products, arithmetic and copies ran while one was open for 0% -> 0% of each run, Pallas kernels for 0% -> 0%
where the time goes in v2:
time: 54.2 us; the launch traced here: 54.1 us
  Pallas kernels  51.7 us (95%)
  local copies, waits for them, and re-layouts  2.39 us (4%)
    pallas_call x1, Pallas kernels, local_layer(): pl.pallas_call(functools.partial(mixer_kernel, n, chunks, ff_tile), name=...  51.7 us
    unnamed x1, local copies, waits for them, and re-layouts  2.39 us

profile of v2, /device:TPU:97, one launch (start us, length us, event | category | flops | bytes accessed | tf_op | source)
XLA Modules:
  0.0 54.1 jit_solution(3631792632526918336)
XLA Ops:
  0.0 51.7 %mixer.1 = bf16[18,64,512]{2,1,0:T(8,128)(2,1)} custom-call(bf16[18,64,512]{2,1,0:T(8,128)(2,1)} %bitcast.12, bf16[18,256]{1,0:T(8,128)(2,1)} %w1_hbm.1, bf16[18,256]{1,0:T(8,128)(2,1)} %bitcast.13, f32[1,8]{1,0:T(1,128)} %bitcast.20, f32[1,18]{1,0:T(1,128)} %bitcast.21, bf16[512,2048]{1,0:T(8,128)(2,1)} %wc1_hbm.1, f32[1,2048]{1,0:T(1,128)} %bitcast.14, ...), custom_call_target="tpu_custom_call" | custom-call | tf_op jit(solution)/shard_map/mixer/pallas_call | solution.py:204
  51.7 2.4 %copy.15 = bf16[64,18,512]{2,0,1:T(8,128)(2,1)} copy(bf16[64,18,512]{2,0,1:T(8,128)(2,1)} %bitcast.11) | data formatting | bytes 2359296

commit v3 on v0

v3 whole, which is shorter than its diff:
```python
import functools
import math

import jax
import jax.numpy as jnp
from jax import lax
from jax.experimental import pallas as pl
from jax.experimental.pallas import tpu as pltpu
from jax.sharding import PartitionSpec as P

LN_EPS = 1e-6
AXIS = "sp"
LANES = 128
CORES = 2
PAIR = 2
VMEM_LIMIT = 67043328
BF16 = jnp.bfloat16
F32 = jnp.float32


def layer_norm(values, ln_gain, ln_bias):
    mean_val = jnp.mean(values, axis=-1, keepdims=True)
    centred = values - mean_val
    var_val = jnp.mean(centred * centred, axis=-1, keepdims=True)
    return centred * lax.rsqrt(var_val + LN_EPS) * ln_gain + ln_bias


def gelu(a):
    return 0.5 * a * (1.0 + jnp.tanh(math.sqrt(2.0 / math.pi) * (a + 0.044715 * (a * a * a))))


def widen(column, copies):
    return jnp.concatenate([column] * copies, axis=1)


def send_order(side):
    hops = lambda d: min(d, side - d)
    flows = []
    for dx, dy in sorted(
        ((dx, dy) for dx in range(side) for dy in range(side) if dx or dy),
        key=lambda o: (hops(o[0]) + hops(o[1]), max(hops(o[0]), hops(o[1])), o),
    ):
        for flow in ((dx, dy), ((side - dx) % side, (side - dy) % side)):
            if flow not in flows:
                flows.append(flow)
    return flows[::-1]


def mixer_kernel(
    n, a_parts, b_parts, b_after, ff_tile,
    x_hbm, w1_hbm, w2_hbm, b1_hbm, b2_hbm, wc1_hbm, bc1_hbm, wc2_hbm, bc2_hbm, g1_hbm, o1_hbm, g2_hbm, o2_hbm,
    out_ref, spare,
    x_own, x_img, z_img, w1_own, w2_own, w1_all, w2_all, w1_t, w2_big, b_own, b_all, b1_col, b2_col, h_mine, h_other, act, wc1, wc2,
    b1_v, b2_v, bc1, bc2, g1, o1, g2, o2, x_tally, w_tally, b_tally,
    local_sem, mine_sem, chan_sem, small_sem, own_sem,
    w_send, w_recv, b_send, b_recv, x_send, x_recv, h_send, h_recv, z_send, z_recv,
):
    me = lax.axis_index(AXIS)
    side = math.isqrt(n // CORES)
    my_core = lax.rem(me, CORES)
    my_chip = me // CORES
    my_x = lax.rem(my_chip, side)
    my_y = my_chip // side
    cols = [lax.rem(my_x + d, side) for d in range(side)]
    lines = [lax.rem(my_y + d, side) * side for d in range(side)]
    chips = [lines[dy] + cols[dx] for dx, dy in send_order(side)]
    other = me + 1 - 2 * my_core
    n_chips = n // CORES
    _, patches, rows, chans = x_img.shape
    pairs = patches // 2
    hid = w1_hbm.shape[1]
    wide = chans // LANES
    ff = wc1.shape[1]

    def two(j):
        return pl.ds(pl.multiple_of(2 * j, 2), 2)

    def image_rows(chip, p):
        return pl.ds(pl.multiple_of(2 * CORES * chip + 2 * p, 2), 2)

    def settle(counted, sem):
        pltpu.make_async_copy(counted, counted, sem).wait()

    def remote(src, dst, ss, rs, j):
        pltpu.make_async_remote_copy(src_ref=src, dst_ref=dst, send_sem=ss, recv_sem=rs, device_id={AXIS: j}).start()

    def to_twins(src, dst, ss, rs):
        for k in chips:
            remote(src(k), dst, ss, rs, CORES * k + my_core)

    b_all[...] = jnp.zeros_like(b_all)
    weights, mine = [], []
    for i, (w_hbm, w_own, w_all) in enumerate(((w1_hbm, w1_own, w1_all), (w2_hbm, w2_own, w2_all))):
        for q in range(pairs):
            src = w_hbm.at[pl.ds(2 * q, 2), :]
            weights.append(pltpu.make_async_copy(src, w_own.at[q], local_sem.at[i, q]))
            mine.append(pltpu.make_async_copy(src, w_all.at[q, two(my_chip), :], mine_sem.at[i, q]))
    x_load = pltpu.make_async_copy(x_hbm, x_own, chan_sem.at[2])
    biases = [pltpu.make_async_copy(b1_hbm, b1_v, small_sem.at[0]), pltpu.make_async_copy(b2_hbm, b2_v, small_sem.at[1])]
    x_mine = [pltpu.make_async_copy(x_hbm.at[:, image_rows(my_chip, p), :], x_img.at[p, :, two(my_chip), :], chan_sem.at[3 + p]) for p in range(PAIR)]
    smalls = [
        pltpu.make_async_copy(src, dst, small_sem.at[2 + i])
        for i, (src, dst) in enumerate(((g1_hbm, g1), (o1_hbm, o1), (g2_hbm, g2), (o2_hbm, o2), (bc1_hbm, bc1), (bc2_hbm, bc2)))
    ]
    chan_loads = [pltpu.make_async_copy(wc1_hbm, wc1, chan_sem.at[0]), pltpu.make_async_copy(wc2_hbm, wc2, chan_sem.at[1])]
    for c in weights + biases + [x_load]:
        c.start()

    barrier = pltpu.get_barrier_semaphore()
    for j in [CORES * k + my_core for k in chips] + [other]:
        pl.semaphore_signal(barrier, inc=1, device_id={AXIS: j})
    for c in mine + x_mine + smalls + chan_loads:
        c.start()
    b_own[...] = jnp.zeros_like(b_own)
    for c in biases:
        c.wait()
    for i, b_v in enumerate((b1_v, b2_v)):
        b_own[i, :, pl.ds(0, b_v.shape[1])] = jnp.broadcast_to(b_v[...], (2, b_v.shape[1]))
    for c in weights + [x_load]:
        c.wait()
    pl.semaphore_wait(barrier, n_chips)

    to_twins(lambda k: w1_own, w1_all.at[:, two(my_chip), :], w_send.at[0], w_recv.at[0])
    to_twins(lambda k: x_own.at[:, image_rows(k, 0), :], x_img.at[0, :, two(my_chip), :], x_send.at[0], x_recv.at[0])
    to_twins(lambda k: b_own, b_all.at[:, two(my_chip), :], b_send, b_recv)
    to_twins(lambda k: w2_own, w2_all.at[:, two(my_chip), :], w_send.at[1], w_recv.at[1])
    to_twins(lambda k: x_own.at[:, image_rows(k, 1), :], x_img.at[1, :, two(my_chip), :], x_send.at[1], x_recv.at[1])

    for c in mine + x_mine + smalls:
        c.wait()

    even = lax.rem(lax.broadcasted_iota(jnp.int32, (rows, hid), 0), 2) == 0
    keep = (lax.rem(lax.broadcasted_iota(jnp.int32, (rows, 2 * hid), 0), 2) == 0) == (
        lax.broadcasted_iota(jnp.int32, (rows, 2 * hid), 1) < hid
    )

    def expand(w_all, q):
        wq = w_all[q].astype(F32)
        first = jnp.where(even, wq, pltpu.roll(wq, 1, 0))
        second = jnp.where(even, pltpu.roll(wq, rows - 1, 0), wq)
        return [jnp.where(keep, jnp.concatenate([d, d], axis=1), 0.0) for d in (first, second)]

    settle(w_tally, w_recv.at[0])
    q = 0
    while q < pairs:
        group = [q] if q + 1 == pairs else [q, q + 1]
        block = jnp.concatenate([d for g in group for d in expand(w1_all, g)], axis=0)
        w1_t[:, pl.ds(2 * rows * q, block.shape[0])] = jnp.transpose(block).astype(BF16)
        q += len(group)

    def half_sum(p):
        settle(x_tally, x_recv.at[p])
        u = layer_norm(x_img[p].reshape(patches * rows, chans).astype(F32), g1[...], o1[...]).astype(BF16)
        for i in range(PAIR):
            span = pl.ds(hid * i, hid)
            h_mine[p, span, :] = jnp.dot(w1_t[span, :], u, preferred_element_type=F32) + widen(b1_col[...], wide)
            remote(h_mine.at[p, span, :], h_other.at[p, span, :], h_send.at[p, i], h_recv.at[p, i], other)

    def activate(p):
        halves = []
        for i in range(PAIR):
            span = pl.ds(hid * i, hid)
            settle(h_other.at[p, span, :], h_recv.at[p, i])
            halves.append(gelu(h_mine[p, span, :] + h_other[p, span, :]).astype(BF16))
        return jnp.concatenate(halves, axis=0)

    def finish(p, g, at, per):
        m = per * rows
        part = pl.ds(at, per)
        span = pl.ds(at * rows, m)
        tok = jnp.dot(w2_big[span, :], g, preferred_element_type=F32) + widen(b2_col[span, :], wide)
        x_mid = (x_img[p, part].reshape(m, chans).astype(F32) + tok).astype(BF16)
        mid_wide = x_mid.astype(F32)
        v = layer_norm(mid_wide, g2[...], o2[...]).astype(BF16)
        for f in range(ff // ff_tile):
            cols_f = pl.ds(f * ff_tile, ff_tile)
            pre = jnp.dot(v, wc1[:, cols_f], preferred_element_type=F32) + bc1[:, cols_f]
            act[pl.ds(0, m), cols_f] = gelu(pre).astype(BF16)
        ch_out = jnp.dot(act[pl.ds(0, m), :], wc2[...], preferred_element_type=F32) + bc2[...]
        z_img[p, part] = (mid_wide + ch_out).astype(BF16).reshape(per, rows, chans)

    def send_back(p, at, per):
        part = pl.ds(at, per)
        out = pltpu.make_async_copy(z_img.at[p, part, two(my_chip), :], spare.at[p, part], own_sem.at[0])
        out.start()
        to_twins(lambda k: z_img.at[p, part, two(k), :], out_ref.at[part, image_rows(my_chip, p), :], z_send.at[p], z_recv.at[p])
        out.wait()
        back = pltpu.make_async_copy(spare.at[p, part], out_ref.at[part, image_rows(my_chip, p), :], own_sem.at[1])
        back.start()
        return back

    settle(b_tally, b_recv)
    is_mine = lax.broadcasted_iota(jnp.int32, (rows, LANES), 0) // 2 == my_chip
    for i in range(2):
        b_all[i] = jnp.where(is_mine, jnp.broadcast_to(b_own[i, pl.ds(0, 1), :], (rows, LANES)), b_all[i])
    per_chip = hid // n_chips
    picked = b_all[0, pl.ds(0, n_chips, stride=2), :]
    spread = jnp.broadcast_to(picked.reshape(n_chips, 1, LANES), (n_chips, per_chip, LANES))
    place = lax.broadcasted_iota(jnp.int32, spread.shape, 1) - (per_chip // CORES) * my_core
    diag = place == lax.broadcasted_iota(jnp.int32, spread.shape, 2)
    col1 = jnp.broadcast_to(jnp.sum(jnp.where(diag, spread, 0.0), axis=2, keepdims=True), spread.shape)
    b1_col[...] = col1.reshape(hid, LANES)
    tail = b_all[1]
    for s in range(patches):
        b2_col[pl.ds(rows * s, rows), :] = jnp.broadcast_to(tail[:, s : s + 1], (rows, LANES))

    half_sum(0)
    settle(w_tally, w_recv.at[1])
    for q in range(pairs):
        w2_big[pl.ds(2 * rows * q, 2 * rows), :] = jnp.concatenate(expand(w2_all, q), axis=0).astype(BF16)
    for c in chan_loads:
        c.wait()

    back = None
    for p, parts in enumerate((a_parts, b_parts)):
        g = activate(p)
        at = 0
        for t, per in enumerate(parts):
            finish(p, g, at, per)
            if back is not None:
                back.wait()
            back = send_back(p, at, per)
            at += per
            if p == 0 and t == b_after:
                half_sum(1)

    back.wait()
    for p in range(PAIR):
        settle(x_tally, z_recv.at[p])
    for p in range(PAIR):
        settle(x_tally, z_send.at[p])
        settle(x_tally, x_send.at[p])
        settle(w_tally, w_send.at[p])
        for i in range(PAIR):
            settle(h_mine.at[p, pl.ds(hid * i, hid), :], h_send.at[p, i])
    settle(b_tally, b_send)


def solution(mesh, a_split=(1, 1), b_split=(4, 3, 2), b_after=0, ff_tile=512):
    row_spec = P("dp", AXIS, None)
    n = mesh.shape[AXIS]

    def local_layer(x_blk, w1_rows, b1_part, w2_cols, b2_part, w_ch1, b_ch1, w_ch2, b_ch2, ln1_gain, ln1_bias, ln2_gain, ln2_bias):
        x_t = jnp.transpose(x_blk, (1, 0, 2))
        w2_rows = jnp.transpose(w2_cols)
        patches, images, chans = x_t.shape
        n_chips = n // CORES
        rows = 2 * n_chips
        hid = w1_rows.shape[1]
        ff = w_ch1.shape[1]
        a_parts = [patches * w // sum(a_split) for w in a_split]
        b_parts = [patches * w // sum(b_split) for w in b_split]
        m = max(a_parts + b_parts) * rows
        hbm = pl.BlockSpec(memory_space=pltpu.HBM)
        sem = pltpu.SemaphoreType.DMA
        smalls = [v[None, :] for v in (b1_part, b2_part, b_ch1, b_ch2, ln1_gain, ln1_bias, ln2_gain, ln2_bias)]
        b1, b2, bc1, bc2, g1, o1, g2, o2 = smalls
        z_t, _ = pl.pallas_call(
            functools.partial(mixer_kernel, n, a_parts, b_parts, b_after, ff_tile),
            name="mixer",
            out_shape=(pltpu.VMEM(x_t.shape, BF16), pltpu.HBM((PAIR, patches, 2, chans), BF16)),
            in_specs=[hbm] * 13,
            out_specs=(pl.BlockSpec(memory_space=pltpu.VMEM), hbm),
            scratch_shapes=[
                pltpu.VMEM(x_t.shape, BF16),
                pltpu.VMEM((PAIR, patches, rows, chans), BF16),
                pltpu.VMEM((PAIR, patches, rows, chans), BF16),
                pltpu.VMEM((patches // 2, 2, hid), BF16),
                pltpu.VMEM((patches // 2, 2, hid), BF16),
                pltpu.VMEM((patches // 2, rows, hid), BF16),
                pltpu.VMEM((patches // 2, rows, hid), BF16),
                pltpu.VMEM((PAIR * hid, patches * rows), BF16),
                pltpu.VMEM((patches * rows, PAIR * hid), BF16),
                pltpu.VMEM((2, 2, LANES), F32),
                pltpu.VMEM((2, rows, LANES), F32),
                pltpu.VMEM((hid, LANES), F32),
                pltpu.VMEM((patches * rows, LANES), F32),
                pltpu.VMEM((PAIR, PAIR * hid, chans), F32),
                pltpu.VMEM((PAIR, PAIR * hid, chans), F32),
                pltpu.VMEM((m, ff), BF16),
                pltpu.VMEM(w_ch1.shape, BF16),
                pltpu.VMEM(w_ch2.shape, BF16),
                *[pltpu.VMEM(v.shape, F32) for v in smalls],
                pltpu.VMEM((n_chips - 1, patches, 2, chans), BF16),
                pltpu.VMEM((n_chips - 1, patches // 2, 2, hid), BF16),
                pltpu.VMEM((n_chips - 1, 2, 2, LANES), F32),
                sem((2, patches // 2)),
                sem((2, patches // 2)),
                sem((5,)),
                sem((8,)),
                sem((2,)),
                sem((2,)), sem((2,)),
                sem, sem,
                sem((PAIR,)), sem((PAIR,)),
                sem((PAIR, PAIR)), sem((PAIR, PAIR)),
                sem((PAIR,)), sem((PAIR,)),
            ],
            compiler_params=pltpu.CompilerParams(
                collective_id=0, has_side_effects=True, vmem_limit_bytes=VMEM_LIMIT - 2 * math.prod(x_t.shape)
            ),
        )(x_t, w1_rows, w2_rows, b1, b2, w_ch1, bc1, w_ch2, bc2, g1, o1, g2, o2)
        return jnp.transpose(z_t, (1, 0, 2))

    in_specs = (row_spec, P(AXIS, None), P(AXIS), P(None, AXIS), P(AXIS), P(None, None), P(None), P(None, None), P(None), P(None), P(None), P(None), P(None))
    return jax.shard_map(local_layer, mesh=mesh, in_specs=in_specs, out_specs=row_spec, check_vma=False)
```

time: 333 us -> 48.4 us (0.15)
  waiting for transfers between devices: 228 us -> 0 us
  Pallas kernels: 0 us -> 47.2 us
  matrix products: 40.7 us -> 0 us
  local copies, waits for them, and re-layouts: 36.1 us -> 1.02 us
  between operations: 13.5 us -> 0.01 us
  other arithmetic: 13.4 us -> 0 us
    reduce_scatter x1 -> x0, waiting for transfers between devices: 160 us -> none  [local_layer(): lax.psum_scatter(part_pre, 'sp', scatter_dimension=1, tiled=True)]
    all_gather x1 -> x0, waiting for transfers between devices: 67.9 us -> none  [local_layer(): act_full = lax.all_gather(tok_act, 'sp', axis=1, tiled=True)]
    pallas_call x0 -> x1, Pallas kernels: none -> 47.2 us  [local_layer(): pl.pallas_call(functools.partial(mixer_kernel, n, a_parts, b_parts, b_aft...]
    dot_general x3 -> x0, matrix products: 40.7 us -> none  [the longest x1 15.9 us: local_layer(): jnp.einsum('bsc,sd->bdc', normed, w1_rows, preferred_element_type=jnp.flo...]
    transpose x1 -> x0, local copies, waits for them, and re-layouts: 34.4 us -> none  [local_layer(): jnp.einsum('bsc,sd->bdc', normed, w1_rows, preferred_element_type=jnp.flo...]
    convert_element_type x3 -> x0, other arithmetic: 8 us -> none  [the longest x1 3.53 us: channel_mix(): return (mid_wide + ch_out).astype(jnp.bfloat16)]
    reduce_sum x3 -> x0, other arithmetic: 5.36 us -> none  [the longest x2 3.18 us: layer_norm(): var_val = jnp.mean(centred * centred, axis=-1, keepdims=True)]
  transfers between devices with their start and end apart: 2 -> 0, of which waited for: 2 -> 0; matrix products, arithmetic and copies ran while one was open for 0% -> 0% of each run, Pallas kernels for 0% -> 0%
where the time goes in v3:
time: 48.4 us; the launch traced here: 48.3 us
  Pallas kernels  47.2 us (98%)
  local copies, waits for them, and re-layouts  1.02 us (2%)
    pallas_call x1, Pallas kernels, local_layer(): pl.pallas_call(functools.partial(mixer_kernel, n, a_parts, b_parts, b_aft...  47.2 us
    unnamed x1, local copies, waits for them, and re-layouts  1.02 us

profile of v3, /device:TPU:97, one launch (start us, length us, event | category | flops | bytes accessed | tf_op | source)
XLA Modules:
  0.0 48.3 jit_solution(12486390304547456943)
XLA Ops:
  0.0 47.2 %mixer.1 = (bf16[18,64,512]{2,1,0:T(8,128)(2,1)S(1)}, bf16[2,18,2,512]{3,2,1,0:T(2,128)(2,1)}) custom-call(bf16[18,64,512]{2,1,0:T(8,128)(2,1)} %bitcast.12, bf16[18,256]{1,0:T(8,128)(2,1)} %w1_hbm.1, bf16[18,256]{1,0:T(8,128)(2,1)} %bitcast.13, f32[1,8]{1,0:T(1,128)} %bitcast.20, f32[1,18]{1,0:T(1,128)} %bitcast.21, bf16[512,2048]{1,0:T(8,128)(2,1)} %wc1_hbm.1, ...), custom_call_target="tpu_custom_call" | custom-call | tf_op jit(solution)/shard_map/mixer/pallas_call | solution.py:258
  47.2 1.0 %copy.15 = bf16[64,18,512]{2,0,1:T(8,128)(2,1)} copy(bf16[64,18,512]{2,0,1:T(8,128)(2,1)S(1)} %bitcast.11) | data formatting | bytes 2359296

commit v4 on v3

--- a/solution.py
+++ b/solution.py
@@ -47,10 +47,10 @@
 
 
 def mixer_kernel(
-    n, a_parts, b_parts, b_after, ff_tile,
+    n, x_parts, z_parts, b_after, ff_tile,
     x_hbm, w1_hbm, w2_hbm, b1_hbm, b2_hbm, wc1_hbm, bc1_hbm, wc2_hbm, bc2_hbm, g1_hbm, o1_hbm, g2_hbm, o2_hbm,
     out_ref, spare,
-    x_own, x_img, z_img, w1_own, w2_own, w1_all, w2_all, w1_t, w2_big, b_own, b_all, b1_col, b2_col, h_mine, h_other, act, wc1, wc2,
+    x_own, x_img, z_img, w1_own, w2_own, w1_all, w2_all, w1_t, w2_big, b_own, b_all, b1_col, b2_col, h_mine, h_other, u_all, v_part, mid_part, act, wc1, wc2,
     b1_v, b2_v, bc1, bc2, g1, o1, g2, o2, x_tally, w_tally, b_tally,
     local_sem, mine_sem, chan_sem, small_sem, own_sem,
     w_send, w_recv, b_send, b_recv, x_send, x_recv, h_send, h_recv, z_send, z_recv,
@@ -120,11 +120,18 @@
         c.wait()
     pl.semaphore_wait(barrier, n_chips)
 
+    def send_x(p):
+        at = 0
+        for t, per in enumerate(x_parts[p]):
+            part = pl.ds(at, per)
+            to_twins(lambda k: x_own.at[part, image_rows(k, p), :], x_img.at[p, part, two(my_chip), :], x_send.at[p], x_recv.at[p, t])
+            at += per
+
     to_twins(lambda k: w1_own, w1_all.at[:, two(my_chip), :], w_send.at[0], w_recv.at[0])
-    to_twins(lambda k: x_own.at[:, image_rows(k, 0), :], x_img.at[0, :, two(my_chip), :], x_send.at[0], x_recv.at[0])
     to_twins(lambda k: b_own, b_all.at[:, two(my_chip), :], b_send, b_recv)
+    send_x(0)
     to_twins(lambda k: w2_own, w2_all.at[:, two(my_chip), :], w_send.at[1], w_recv.at[1])
-    to_twins(lambda k: x_own.at[:, image_rows(k, 1), :], x_img.at[1, :, two(my_chip), :], x_send.at[1], x_recv.at[1])
+    send_x(1)
 
     for c in mine + x_mine + smalls:
         c.wait()
@@ -149,8 +156,13 @@
         q += len(group)
 
     def half_sum(p):
-        settle(x_tally, x_recv.at[p])
-        u = layer_norm(x_img[p].reshape(patches * rows, chans).astype(F32), g1[...], o1[...]).astype(BF16)
+        at = 0
+        for t, per in enumerate(x_parts[p]):
+            settle(x_tally.at[:, pl.ds(0, per)], x_recv.at[p, t])
+            wide_x = x_img[p, pl.ds(at, per)].reshape(per * rows, chans).astype(F32)
+            u_all[pl.ds(at * rows, per * rows), :] = layer_norm(wide_x, g1[...], o1[...]).astype(BF16)
+            at += per
+        u = u_all[...]
         for i in range(PAIR):
             span = pl.ds(hid * i, hid)
             h_mine[p, span, :] = jnp.dot(w1_t[span, :], u, preferred_element_type=F32) + widen(b1_col[...], wide)
@@ -164,30 +176,32 @@
             halves.append(gelu(h_mine[p, span, :] + h_other[p, span, :]).astype(BF16))
         return jnp.concatenate(halves, axis=0)
 
-    def finish(p, g, at, per):
+    def prepare(slot, p, g, at, per):
         m = per * rows
-        part = pl.ds(at, per)
         span = pl.ds(at * rows, m)
         tok = jnp.dot(w2_big[span, :], g, preferred_element_type=F32) + widen(b2_col[span, :], wide)
-        x_mid = (x_img[p, part].reshape(m, chans).astype(F32) + tok).astype(BF16)
-        mid_wide = x_mid.astype(F32)
-        v = layer_norm(mid_wide, g2[...], o2[...]).astype(BF16)
+        x_mid = (x_img[p, pl.ds(at, per)].reshape(m, chans).astype(F32) + tok).astype(BF16)
+        mid_part[slot, pl.ds(0, m), :] = x_mid
+        v_part[slot, pl.ds(0, m), :] = layer_norm(x_mid.astype(F32), g2[...], o2[...]).astype(BF16)
+
+    def expand_channels(slot, per):
+        m = pl.ds(0, per * rows)
+        v = v_part[slot, m, :]
         for f in range(ff // ff_tile):
             cols_f = pl.ds(f * ff_tile, ff_tile)
             pre = jnp.dot(v, wc1[:, cols_f], preferred_element_type=F32) + bc1[:, cols_f]
-            act[pl.ds(0, m), cols_f] = gelu(pre).astype(BF16)
-        ch_out = jnp.dot(act[pl.ds(0, m), :], wc2[...], preferred_element_type=F32) + bc2[...]
-        z_img[p, part] = (mid_wide + ch_out).astype(BF16).reshape(per, rows, chans)
-
-    def send_back(p, at, per):
+            act[m, cols_f] = gelu(pre).astype(BF16)
+
+    def contract_channels(slot, p, at, per):
+        m = pl.ds(0, per * rows)
+        ch_out = jnp.dot(act[m, :], wc2[...], preferred_element_type=F32) + bc2[...]
+        z_img[p, pl.ds(at, per)] = (mid_part[slot, m, :].astype(F32) + ch_out).astype(BF16).reshape(per, rows, chans)
+
+    def own_block(i, p, at, per):
         part = pl.ds(at, per)
-        out = pltpu.make_async_copy(z_img.at[p, part, two(my_chip), :], spare.at[p, part], own_sem.at[0])
-        out.start()
-        to_twins(lambda k: z_img.at[p, part, two(k), :], out_ref.at[part, image_rows(my_chip, p), :], z_send.at[p], z_recv.at[p])
-        out.wait()
-        back = pltpu.make_async_copy(spare.at[p, part], out_ref.at[part, image_rows(my_chip, p), :], own_sem.at[1])
-        back.start()
-        return back
+        away = pltpu.make_async_copy(z_img.at[p, part, two(my_chip), :], spare.at[p, part], own_sem.at[0, i])
+        back = pltpu.make_async_copy(spare.at[p, part], out_ref.at[part, image_rows(my_chip, p), :], own_sem.at[1, i])
+        return away, back
 
     settle(b_tally, b_recv)
     is_mine = lax.broadcasted_iota(jnp.int32, (rows, LANES), 0) // 2 == my_chip
@@ -211,20 +225,33 @@
     for c in chan_loads:
         c.wait()
 
-    back = None
-    for p, parts in enumerate((a_parts, b_parts)):
-        g = activate(p)
-        at = 0
-        for t, per in enumerate(parts):
-            finish(p, g, at, per)
-            if back is not None:
-                back.wait()
-            back = send_back(p, at, per)
-            at += per
-            if p == 0 and t == b_after:
-                half_sum(1)
-
-    back.wait()
+    steps = [(p, sum(parts[:t]), per) for p, parts in enumerate(z_parts) for t, per in enumerate(parts)]
+    g = activate(0)
+    prepare(0, 0, g, *steps[0][1:])
+    own = []
+    for i, (p, at, per) in enumerate(steps):
+        slot = i % 2
+        part = pl.ds(at, per)
+        expand_channels(slot, per)
+        if i + 1 < len(steps):
+            following = steps[i + 1]
+            if following[0] != p:
+                g = activate(following[0])
+            prepare(1 - slot, following[0], g, *following[1:])
+        contract_channels(slot, p, at, per)
+        if own:
+            own[-1][0].wait()
+            own[-1][1].start()
+        own.append(own_block(i, p, at, per))
+        own[-1][0].start()
+        to_twins(lambda k: z_img.at[p, part, two(k), :], out_ref.at[part, image_rows(my_chip, p), :], z_send.at[p], z_recv.at[p])
+        if i == b_after:
+            half_sum(1)
+
+    own[-1][0].wait()
+    own[-1][1].start()
+    for _, back in own:
+        back.wait()
     for p in range(PAIR):
         settle(x_tally, z_recv.at[p])
     for p in range(PAIR):
@@ -236,7 +263,7 @@
     settle(b_tally, b_send)
 
 
-def solution(mesh, a_split=(1, 1), b_split=(4, 3, 2), b_after=0, ff_tile=512):
+def solution(mesh, x_split=((1, 1), (1,)), z_split=((1, 1), (4, 3, 2)), b_after=0, ff_tile=512):
     row_spec = P("dp", AXIS, None)
     n = mesh.shape[AXIS]
 
@@ -248,15 +275,14 @@
         rows = 2 * n_chips
         hid = w1_rows.shape[1]
         ff = w_ch1.shape[1]
-        a_parts = [patches * w // sum(a_split) for w in a_split]
-        b_parts = [patches * w // sum(b_split) for w in b_split]
-        m = max(a_parts + b_parts) * rows
+        x_parts, z_parts = ([[patches * w // sum(ws) for w in ws] for ws in split] for split in (x_split, z_split))
+        m = max(max(parts) for parts in z_parts) * rows
         hbm = pl.BlockSpec(memory_space=pltpu.HBM)
         sem = pltpu.SemaphoreType.DMA
         smalls = [v[None, :] for v in (b1_part, b2_part, b_ch1, b_ch2, ln1_gain, ln1_bias, ln2_gain, ln2_bias)]
         b1, b2, bc1, bc2, g1, o1, g2, o2 = smalls
         z_t, _ = pl.pallas_call(
-            functools.partial(mixer_kernel, n, a_parts, b_parts, b_after, ff_tile),
+            functools.partial(mixer_kernel, n, x_parts, z_parts, b_after, ff_tile),
             name="mixer",
             out_shape=(pltpu.VMEM(x_t.shape, BF16), pltpu.HBM((PAIR, patches, 2, chans), BF16)),
             in_specs=[hbm] * 13,
@@ -277,6 +303,9 @@
                 pltpu.VMEM((patches * rows, LANES), F32),
                 pltpu.VMEM((PAIR, PAIR * hid, chans), F32),
                 pltpu.VMEM((PAIR, PAIR * hid, chans), F32),
+                pltpu.VMEM((patches * rows, chans), BF16),
+                pltpu.VMEM((2, m, chans), BF16),
+                pltpu.VMEM((2, m, chans), BF16),
                 pltpu.VMEM((m, ff), BF16),
                 pltpu.VMEM(w_ch1.shape, BF16),
                 pltpu.VMEM(w_ch2.shape, BF16),
@@ -288,10 +317,10 @@
                 sem((2, patches // 2)),
                 sem((5,)),
                 sem((8,)),
-                sem((2,)),
+                sem((2, sum(len(parts) for parts in z_parts))),
                 sem((2,)), sem((2,)),
                 sem, sem,
-                sem((PAIR,)), sem((PAIR,)),
+                sem((PAIR,)), sem((PAIR, max(len(parts) for parts in x_parts))),
                 sem((PAIR, PAIR)), sem((PAIR, PAIR)),
                 sem((PAIR,)), sem((PAIR,)),
             ],

time: 48.4 us -> 48.1 us (level)
  no operation moved by 1% of the time
where the time goes in v4:
time: 48.1 us; the launch traced here: 47.9 us
  Pallas kernels  46.9 us (98%)
  local copies, waits for them, and re-layouts  1.02 us (2%)
    pallas_call x1, Pallas kernels, local_layer(): pl.pallas_call(functools.partial(mixer_kernel, n, x_parts, z_parts, b_aft...  46.9 us
    unnamed x1, local copies, waits for them, and re-layouts  1.02 us

profile of v4, /device:TPU:97, one launch (start us, length us, event | category | flops | bytes accessed | tf_op | source)
XLA Modules:
  0.0 47.9 jit_solution(10785076654872290062)
XLA Ops:
  0.0 46.9 %mixer.1 = (bf16[18,64,512]{2,1,0:T(8,128)(2,1)S(1)}, bf16[2,18,2,512]{3,2,1,0:T(2,128)(2,1)}) custom-call(bf16[18,64,512]{2,1,0:T(8,128)(2,1)} %bitcast.12, bf16[18,256]{1,0:T(8,128)(2,1)} %w1_hbm.1, bf16[18,256]{1,0:T(8,128)(2,1)} %bitcast.13, f32[1,8]{1,0:T(1,128)} %bitcast.20, f32[1,18]{1,0:T(1,128)} %bitcast.21, bf16[512,2048]{1,0:T(8,128)(2,1)} %wc1_hbm.1, ...), custom_call_target="tpu_custom_call" | custom-call | tf_op jit(solution)/shard_map/mixer/pallas_call | solution.py:284
  46.9 1.0 %copy.15 = bf16[64,18,512]{2,0,1:T(8,128)(2,1)} copy(bf16[64,18,512]{2,0,1:T(8,128)(2,1)S(1)} %bitcast.11) | data formatting | bytes 2359296

commit v5 on v4

--- a/solution.py
+++ b/solution.py
@@ -50,7 +50,7 @@
     n, x_parts, z_parts, b_after, ff_tile,
     x_hbm, w1_hbm, w2_hbm, b1_hbm, b2_hbm, wc1_hbm, bc1_hbm, wc2_hbm, bc2_hbm, g1_hbm, o1_hbm, g2_hbm, o2_hbm,
     out_ref, spare,
-    x_own, x_img, z_img, w1_own, w2_own, w1_all, w2_all, w1_t, w2_big, b_own, b_all, b1_col, b2_col, h_mine, h_other, u_all, v_part, mid_part, act, wc1, wc2,
+    x_own, x_img, z_img, w1_own, w2_own, w1_all, w2_all, w1_t, w2_big, b_own, b_all, b1_col, b2_col, h_mine, h_other, v_part, mid_part, act, wc1, wc2,
     b1_v, b2_v, bc1, bc2, g1, o1, g2, o2, x_tally, w_tally, b_tally,
     local_sem, mine_sem, chan_sem, small_sem, own_sem,
     w_send, w_recv, b_send, b_recv, x_send, x_recv, h_send, h_recv, z_send, z_recv,
@@ -64,6 +64,8 @@
     cols = [lax.rem(my_x + d, side) for d in range(side)]
     lines = [lax.rem(my_y + d, side) * side for d in range(side)]
     chips = [lines[dy] + cols[dx] for dx, dy in send_order(side)]
+    row_chips = [lines[0] + cols[dx] for dx, dy in send_order(side) if dy == 0]
+    col_chips = [lines[dy] + cols[0] for dx, dy in send_order(side) if dx == 0]
     other = me + 1 - 2 * my_core
     n_chips = n // CORES
     _, patches, rows, chans = x_img.shape
@@ -84,8 +86,8 @@
     def remote(src, dst, ss, rs, j):
         pltpu.make_async_remote_copy(src_ref=src, dst_ref=dst, send_sem=ss, recv_sem=rs, device_id={AXIS: j}).start()
 
-    def to_twins(src, dst, ss, rs):
-        for k in chips:
+    def to_twins(src, dst, ss, rs, targets=chips):
+        for k in targets:
             remote(src(k), dst, ss, rs, CORES * k + my_core)
 
     b_all[...] = jnp.zeros_like(b_all)
@@ -120,21 +122,29 @@
         c.wait()
     pl.semaphore_wait(barrier, n_chips)
 
-    def send_x(p):
-        at = 0
-        for t, per in enumerate(x_parts[p]):
-            part = pl.ds(at, per)
-            to_twins(lambda k: x_own.at[part, image_rows(k, p), :], x_img.at[p, part, two(my_chip), :], x_send.at[p], x_recv.at[p, t])
-            at += per
-
-    to_twins(lambda k: w1_own, w1_all.at[:, two(my_chip), :], w_send.at[0], w_recv.at[0])
+    def send_x(p, t):
+        part = pl.ds(sum(x_parts[p][:t]), x_parts[p][t])
+        to_twins(lambda k: x_own.at[part, image_rows(k, p), :], x_img.at[p, part, two(my_chip), :], x_send.at[p], x_recv.at[p, t])
+
+    to_twins(lambda k: w1_own, w1_all.at[:, two(my_chip), :], w_send.at[0], w_recv.at[0, 0], row_chips)
+    to_twins(lambda k: w2_own, w2_all.at[:, two(my_chip), :], w_send.at[1], w_recv.at[1, 0], col_chips)
     to_twins(lambda k: b_own, b_all.at[:, two(my_chip), :], b_send, b_recv)
-    send_x(0)
-    to_twins(lambda k: w2_own, w2_all.at[:, two(my_chip), :], w_send.at[1], w_recv.at[1])
-    send_x(1)
-
+    send_x(0, 0)
     for c in mine + x_mine + smalls:
         c.wait()
+    near = w_tally.at[pl.ds(0, side - 1)]
+    far = w_tally.at[pl.ds(0, side * (side - 1))]
+    line = w1_all.at[:, pl.ds(pl.multiple_of(2 * side * my_y, 2 * side), 2 * side), :]
+    settle(near, w_recv.at[0, 0])
+    to_twins(lambda k: line, line, w_send.at[0], w_recv.at[0, 1], col_chips)
+    settle(near, w_recv.at[1, 0])
+    for c in [my_chip] + col_chips:
+        block = w2_all.at[:, two(c), :]
+        to_twins(lambda k: block, block, w_send.at[1], w_recv.at[1, 1], row_chips)
+    for t in range(1, len(x_parts[0])):
+        send_x(0, t)
+    for t in range(len(x_parts[1])):
+        send_x(1, t)
 
     even = lax.rem(lax.broadcasted_iota(jnp.int32, (rows, hid), 0), 2) == 0
     keep = (lax.rem(lax.broadcasted_iota(jnp.int32, (rows, 2 * hid), 0), 2) == 0) == (
@@ -147,7 +157,7 @@
         second = jnp.where(even, pltpu.roll(wq, rows - 1, 0), wq)
         return [jnp.where(keep, jnp.concatenate([d, d], axis=1), 0.0) for d in (first, second)]
 
-    settle(w_tally, w_recv.at[0])
+    settle(far, w_recv.at[0, 1])
     q = 0
     while q < pairs:
         group = [q] if q + 1 == pairs else [q, q + 1]
@@ -160,13 +170,14 @@
         for t, per in enumerate(x_parts[p]):
             settle(x_tally.at[:, pl.ds(0, per)], x_recv.at[p, t])
             wide_x = x_img[p, pl.ds(at, per)].reshape(per * rows, chans).astype(F32)
-            u_all[pl.ds(at * rows, per * rows), :] = layer_norm(wide_x, g1[...], o1[...]).astype(BF16)
+            u = layer_norm(wide_x, g1[...], o1[...]).astype(BF16)
+            for i in range(PAIR):
+                span = pl.ds(hid * i, hid)
+                before = h_mine[p, span, :] if t else widen(b1_col[...], wide)
+                h_mine[p, span, :] = before + jnp.dot(w1_t[span, pl.ds(at * rows, per * rows)], u, preferred_element_type=F32)
+                if t == len(x_parts[p]) - 1:
+                    remote(h_mine.at[p, span, :], h_other.at[p, span, :], h_send.at[p, i], h_recv.at[p, i], other)
             at += per
-        u = u_all[...]
-        for i in range(PAIR):
-            span = pl.ds(hid * i, hid)
-            h_mine[p, span, :] = jnp.dot(w1_t[span, :], u, preferred_element_type=F32) + widen(b1_col[...], wide)
-            remote(h_mine.at[p, span, :], h_other.at[p, span, :], h_send.at[p, i], h_recv.at[p, i], other)
 
     def activate(p):
         halves = []
@@ -218,10 +229,10 @@
     for s in range(patches):
         b2_col[pl.ds(rows * s, rows), :] = jnp.broadcast_to(tail[:, s : s + 1], (rows, LANES))
 
-    half_sum(0)
-    settle(w_tally, w_recv.at[1])
+    settle(far, w_recv.at[1, 1])
     for q in range(pairs):
         w2_big[pl.ds(2 * rows * q, 2 * rows), :] = jnp.concatenate(expand(w2_all, q), axis=0).astype(BF16)
+    half_sum(0)
     for c in chan_loads:
         c.wait()
 
@@ -233,8 +244,8 @@
         slot = i % 2
         part = pl.ds(at, per)
         expand_channels(slot, per)
-        if i + 1 < len(steps):
-            following = steps[i + 1]
+        following = steps[i + 1] if i + 1 < len(steps) else None
+        if following and i:
             if following[0] != p:
                 g = activate(following[0])
             prepare(1 - slot, following[0], g, *following[1:])
@@ -245,6 +256,8 @@
         own.append(own_block(i, p, at, per))
         own[-1][0].start()
         to_twins(lambda k: z_img.at[p, part, two(k), :], out_ref.at[part, image_rows(my_chip, p), :], z_send.at[p], z_recv.at[p])
+        if i == 0:
+            prepare(1 - slot, p, g, *following[1:])
         if i == b_after:
             half_sum(1)
 
@@ -263,7 +276,7 @@
     settle(b_tally, b_send)
 
 
-def solution(mesh, x_split=((1, 1), (1,)), z_split=((1, 1), (4, 3, 2)), b_after=0, ff_tile=512):
+def solution(mesh, x_split=((1, 1), (1,)), z_split=((1, 2, 3), (4, 3, 2)), b_after=1, ff_tile=512):
     row_spec = P("dp", AXIS, None)
     n = mesh.shape[AXIS]
 
@@ -303,7 +316,6 @@
                 pltpu.VMEM((patches * rows, LANES), F32),
                 pltpu.VMEM((PAIR, PAIR * hid, chans), F32),
                 pltpu.VMEM((PAIR, PAIR * hid, chans), F32),
-                pltpu.VMEM((patches * rows, chans), BF16),
                 pltpu.VMEM((2, m, chans), BF16),
                 pltpu.VMEM((2, m, chans), BF16),
                 pltpu.VMEM((m, ff), BF16),
@@ -318,7 +330,7 @@
                 sem((5,)),
                 sem((8,)),
                 sem((2, sum(len(parts) for parts in z_parts))),
-                sem((2,)), sem((2,)),
+                sem((2,)), sem((2, 2)),
                 sem, sem,
                 sem((PAIR,)), sem((PAIR, max(len(parts) for parts in x_parts))),
                 sem((PAIR, PAIR)), sem((PAIR, PAIR)),

time: 48.1 us -> 48.2 us (level)
  no operation moved by 1% of the time
where the time goes in v5:
time: 48.2 us; the launch traced here: 48.1 us
  Pallas kernels  47 us (98%)
  local copies, waits for them, and re-layouts  1.02 us (2%)
    pallas_call x1, Pallas kernels, local_layer(): pl.pallas_call(functools.partial(mixer_kernel, n, x_parts, z_parts, b_aft...  47 us
    unnamed x1, local copies, waits for them, and re-layouts  1.02 us

profile of v5, /device:TPU:97, one launch (start us, length us, event | category | flops | bytes accessed | tf_op | source)
XLA Modules:
  0.0 48.1 jit_solution(5202974365094025897)
XLA Ops:
  0.0 47.0 %mixer.1 = (bf16[18,64,512]{2,1,0:T(8,128)(2,1)S(1)}, bf16[2,18,2,512]{3,2,1,0:T(2,128)(2,1)}) custom-call(bf16[18,64,512]{2,1,0:T(8,128)(2,1)} %bitcast.12, bf16[18,256]{1,0:T(8,128)(2,1)} %w1_hbm.1, bf16[18,256]{1,0:T(8,128)(2,1)} %bitcast.13, f32[1,8]{1,0:T(1,128)} %bitcast.20, f32[1,18]{1,0:T(1,128)} %bitcast.21, bf16[512,2048]{1,0:T(8,128)(2,1)} %wc1_hbm.1, ...), custom_call_target="tpu_custom_call" | custom-call | tf_op jit(solution)/shard_map/mixer/pallas_call | solution.py:297
  47.0 1.0 %copy.15 = bf16[64,18,512]{2,0,1:T(8,128)(2,1)} copy(bf16[64,18,512]{2,0,1:T(8,128)(2,1)S(1)} %bitcast.11) | data formatting | bytes 2359296

commit v6 on v5

--- a/solution.py
+++ b/solution.py
@@ -13,6 +13,7 @@
 LANES = 128
 CORES = 2
 PAIR = 2
+SWAPS = 4
 VMEM_LIMIT = 67043328
 BF16 = jnp.bfloat16
 F32 = jnp.float32
@@ -73,6 +74,7 @@
     hid = w1_hbm.shape[1]
     wide = chans // LANES
     ff = wc1.shape[1]
+    piece = PAIR * hid // SWAPS
 
     def two(j):
         return pl.ds(pl.multiple_of(2 * j, 2), 2)
@@ -91,6 +93,11 @@
             remote(src(k), dst, ss, rs, CORES * k + my_core)
 
     b_all[...] = jnp.zeros_like(b_all)
+
+    barrier = pltpu.get_barrier_semaphore()
+    for j in [CORES * k + my_core for k in chips] + [other]:
+        pl.semaphore_signal(barrier, inc=1, device_id={AXIS: j})
+
     weights, mine = [], []
     for i, (w_hbm, w_own, w_all) in enumerate(((w1_hbm, w1_own, w1_all), (w2_hbm, w2_own, w2_all))):
         for q in range(pairs):
@@ -105,13 +112,7 @@
         for i, (src, dst) in enumerate(((g1_hbm, g1), (o1_hbm, o1), (g2_hbm, g2), (o2_hbm, o2), (bc1_hbm, bc1), (bc2_hbm, bc2)))
     ]
     chan_loads = [pltpu.make_async_copy(wc1_hbm, wc1, chan_sem.at[0]), pltpu.make_async_copy(wc2_hbm, wc2, chan_sem.at[1])]
-    for c in weights + biases + [x_load]:
-        c.start()
-
-    barrier = pltpu.get_barrier_semaphore()
-    for j in [CORES * k + my_core for k in chips] + [other]:
-        pl.semaphore_signal(barrier, inc=1, device_id={AXIS: j})
-    for c in mine + x_mine + smalls + chan_loads:
+    for c in weights + biases + [x_load] + mine + x_mine + smalls + chan_loads:
         c.start()
     b_own[...] = jnp.zeros_like(b_own)
     for c in biases:
@@ -137,12 +138,12 @@
     line = w1_all.at[:, pl.ds(pl.multiple_of(2 * side * my_y, 2 * side), 2 * side), :]
     settle(near, w_recv.at[0, 0])
     to_twins(lambda k: line, line, w_send.at[0], w_recv.at[0, 1], col_chips)
+    for t in range(1, len(x_parts[0])):
+        send_x(0, t)
     settle(near, w_recv.at[1, 0])
     for c in [my_chip] + col_chips:
         block = w2_all.at[:, two(c), :]
         to_twins(lambda k: block, block, w_send.at[1], w_recv.at[1, 1], row_chips)
-    for t in range(1, len(x_parts[0])):
-        send_x(0, t)
     for t in range(len(x_parts[1])):
         send_x(1, t)
 
@@ -171,9 +172,9 @@
             settle(x_tally.at[:, pl.ds(0, per)], x_recv.at[p, t])
             wide_x = x_img[p, pl.ds(at, per)].reshape(per * rows, chans).astype(F32)
             u = layer_norm(wide_x, g1[...], o1[...]).astype(BF16)
-            for i in range(PAIR):
-                span = pl.ds(hid * i, hid)
-                before = h_mine[p, span, :] if t else widen(b1_col[...], wide)
+            for i in range(SWAPS):
+                span = pl.ds(piece * i, piece)
+                before = h_mine[p, span, :] if t else widen(b1_col[pl.ds(piece * i % hid, piece), :], wide)
                 h_mine[p, span, :] = before + jnp.dot(w1_t[span, pl.ds(at * rows, per * rows)], u, preferred_element_type=F32)
                 if t == len(x_parts[p]) - 1:
                     remote(h_mine.at[p, span, :], h_other.at[p, span, :], h_send.at[p, i], h_recv.at[p, i], other)
@@ -181,8 +182,8 @@
 
     def activate(p):
         halves = []
-        for i in range(PAIR):
-            span = pl.ds(hid * i, hid)
+        for i in range(SWAPS):
+            span = pl.ds(piece * i, piece)
             settle(h_other.at[p, span, :], h_recv.at[p, i])
             halves.append(gelu(h_mine[p, span, :] + h_other[p, span, :]).astype(BF16))
         return jnp.concatenate(halves, axis=0)
@@ -229,10 +230,10 @@
     for s in range(patches):
         b2_col[pl.ds(rows * s, rows), :] = jnp.broadcast_to(tail[:, s : s + 1], (rows, LANES))
 
+    half_sum(0)
     settle(far, w_recv.at[1, 1])
     for q in range(pairs):
         w2_big[pl.ds(2 * rows * q, 2 * rows), :] = jnp.concatenate(expand(w2_all, q), axis=0).astype(BF16)
-    half_sum(0)
     for c in chan_loads:
         c.wait()
 
@@ -271,12 +272,12 @@
         settle(x_tally, z_send.at[p])
         settle(x_tally, x_send.at[p])
         settle(w_tally, w_send.at[p])
-        for i in range(PAIR):
-            settle(h_mine.at[p, pl.ds(hid * i, hid), :], h_send.at[p, i])
+        for i in range(SWAPS):
+            settle(h_mine.at[p, pl.ds(piece * i, piece), :], h_send.at[p, i])
     settle(b_tally, b_send)
 
 
-def solution(mesh, x_split=((1, 1), (1,)), z_split=((1, 2, 3), (4, 3, 2)), b_after=1, ff_tile=512):
+def solution(mesh, x_split=((4, 3, 2), (1,)), z_split=((2, 1), (4, 3, 2)), b_after=0, ff_tile=512):
     row_spec = P("dp", AXIS, None)
     n = mesh.shape[AXIS]
 
@@ -333,7 +334,7 @@
                 sem((2,)), sem((2, 2)),
                 sem, sem,
                 sem((PAIR,)), sem((PAIR, max(len(parts) for parts in x_parts))),
-                sem((PAIR, PAIR)), sem((PAIR, PAIR)),
+                sem((PAIR, SWAPS)), sem((PAIR, SWAPS)),
                 sem((PAIR,)), sem((PAIR,)),
             ],
             compiler_params=pltpu.CompilerParams(

time: 48.2 us -> 45 us (0.934)
  Pallas kernels: 47 us -> 43.8 us
    pallas_call x1, Pallas kernels: 47 us -> 43.8 us  [local_layer(): pl.pallas_call(functools.partial(mixer_kernel, n, x_parts, z_parts, b_aft...]
where the time goes in v6:
time: 45 us; the launch traced here: 44.8 us
  Pallas kernels  43.8 us (97%)
  local copies, waits for them, and re-layouts  1.02 us (2%)
    pallas_call x1, Pallas kernels, local_layer(): pl.pallas_call(functools.partial(mixer_kernel, n, x_parts, z_parts, b_aft...  43.8 us
    unnamed x1, local copies, waits for them, and re-layouts  1.02 us

profile of v6, /device:TPU:97, one launch (start us, length us, event | category | flops | bytes accessed | tf_op | source)
XLA Modules:
  0.0 44.8 jit_solution(9228542039291042581)
XLA Ops:
  0.0 43.8 %mixer.1 = (bf16[18,64,512]{2,1,0:T(8,128)(2,1)S(1)}, bf16[2,18,2,512]{3,2,1,0:T(2,128)(2,1)}) custom-call(bf16[18,64,512]{2,1,0:T(8,128)(2,1)} %bitcast.12, bf16[18,256]{1,0:T(8,128)(2,1)} %w1_hbm.1, bf16[18,256]{1,0:T(8,128)(2,1)} %bitcast.13, f32[1,8]{1,0:T(1,128)} %bitcast.20, f32[1,18]{1,0:T(1,128)} %bitcast.21, bf16[512,2048]{1,0:T(8,128)(2,1)} %wc1_hbm.1, ...), custom_call_target="tpu_custom_call" | custom-call | tf_op jit(solution)/shard_map/mixer/pallas_call | solution.py:298
  43.8 1.0 %copy.15 = bf16[64,18,512]{2,0,1:T(8,128)(2,1)} copy(bf16[64,18,512]{2,0,1:T(8,128)(2,1)S(1)} %bitcast.11) | data formatting | bytes 2359296

commit v7 on v6

--- a/solution.py
+++ b/solution.py
@@ -27,7 +27,9 @@
 
 
 def gelu(a):
-    return 0.5 * a * (1.0 + jnp.tanh(math.sqrt(2.0 / math.pi) * (a + 0.044715 * (a * a * a))))
+    scale = math.sqrt(2.0 / math.pi)
+    half = 0.5 * a
+    return half + half * jnp.tanh(a * (scale + (scale * 0.044715) * (a * a)))
 
 
 def widen(column, copies):
@@ -65,8 +67,6 @@
     cols = [lax.rem(my_x + d, side) for d in range(side)]
     lines = [lax.rem(my_y + d, side) * side for d in range(side)]
     chips = [lines[dy] + cols[dx] for dx, dy in send_order(side)]
-    row_chips = [lines[0] + cols[dx] for dx, dy in send_order(side) if dy == 0]
-    col_chips = [lines[dy] + cols[0] for dx, dy in send_order(side) if dx == 0]
     other = me + 1 - 2 * my_core
     n_chips = n // CORES
     _, patches, rows, chans = x_img.shape
@@ -88,8 +88,8 @@
     def remote(src, dst, ss, rs, j):
         pltpu.make_async_remote_copy(src_ref=src, dst_ref=dst, send_sem=ss, recv_sem=rs, device_id={AXIS: j}).start()
 
-    def to_twins(src, dst, ss, rs, targets=chips):
-        for k in targets:
+    def to_twins(src, dst, ss, rs):
+        for k in chips:
             remote(src(k), dst, ss, rs, CORES * k + my_core)
 
     b_all[...] = jnp.zeros_like(b_all)
@@ -112,14 +112,15 @@
         for i, (src, dst) in enumerate(((g1_hbm, g1), (o1_hbm, o1), (g2_hbm, g2), (o2_hbm, o2), (bc1_hbm, bc1), (bc2_hbm, bc2)))
     ]
     chan_loads = [pltpu.make_async_copy(wc1_hbm, wc1, chan_sem.at[0]), pltpu.make_async_copy(wc2_hbm, wc2, chan_sem.at[1])]
-    for c in weights + biases + [x_load] + mine + x_mine + smalls + chan_loads:
+    early_weights, late_weights = weights[:pairs], weights[pairs:]
+    for c in [x_load] + early_weights + biases + late_weights + mine + x_mine + smalls + chan_loads:
         c.start()
     b_own[...] = jnp.zeros_like(b_own)
     for c in biases:
         c.wait()
     for i, b_v in enumerate((b1_v, b2_v)):
         b_own[i, :, pl.ds(0, b_v.shape[1])] = jnp.broadcast_to(b_v[...], (2, b_v.shape[1]))
-    for c in weights + [x_load]:
+    for c in early_weights + [x_load]:
         c.wait()
     pl.semaphore_wait(barrier, n_chips)
 
@@ -127,25 +128,17 @@
         part = pl.ds(sum(x_parts[p][:t]), x_parts[p][t])
         to_twins(lambda k: x_own.at[part, image_rows(k, p), :], x_img.at[p, part, two(my_chip), :], x_send.at[p], x_recv.at[p, t])
 
-    to_twins(lambda k: w1_own, w1_all.at[:, two(my_chip), :], w_send.at[0], w_recv.at[0, 0], row_chips)
-    to_twins(lambda k: w2_own, w2_all.at[:, two(my_chip), :], w_send.at[1], w_recv.at[1, 0], col_chips)
+    to_twins(lambda k: w1_own, w1_all.at[:, two(my_chip), :], w_send.at[0], w_recv.at[0])
     to_twins(lambda k: b_own, b_all.at[:, two(my_chip), :], b_send, b_recv)
-    send_x(0, 0)
-    for c in mine + x_mine + smalls:
-        c.wait()
-    near = w_tally.at[pl.ds(0, side - 1)]
-    far = w_tally.at[pl.ds(0, side * (side - 1))]
-    line = w1_all.at[:, pl.ds(pl.multiple_of(2 * side * my_y, 2 * side), 2 * side), :]
-    settle(near, w_recv.at[0, 0])
-    to_twins(lambda k: line, line, w_send.at[0], w_recv.at[0, 1], col_chips)
-    for t in range(1, len(x_parts[0])):
+    for t in range(len(x_parts[0])):
         send_x(0, t)
-    settle(near, w_recv.at[1, 0])
-    for c in [my_chip] + col_chips:
-        block = w2_all.at[:, two(c), :]
-        to_twins(lambda k: block, block, w_send.at[1], w_recv.at[1, 1], row_chips)
+    for c in late_weights:
+        c.wait()
+    to_twins(lambda k: w2_own, w2_all.at[:, two(my_chip), :], w_send.at[1], w_recv.at[1])
     for t in range(len(x_parts[1])):
         send_x(1, t)
+    for c in mine + x_mine + smalls:
+        c.wait()
 
     even = lax.rem(lax.broadcasted_iota(jnp.int32, (rows, hid), 0), 2) == 0
     keep = (lax.rem(lax.broadcasted_iota(jnp.int32, (rows, 2 * hid), 0), 2) == 0) == (
@@ -158,7 +151,7 @@
         second = jnp.where(even, pltpu.roll(wq, rows - 1, 0), wq)
         return [jnp.where(keep, jnp.concatenate([d, d], axis=1), 0.0) for d in (first, second)]
 
-    settle(far, w_recv.at[0, 1])
+    settle(w_tally, w_recv.at[0])
     q = 0
     while q < pairs:
         group = [q] if q + 1 == pairs else [q, q + 1]
@@ -172,12 +165,16 @@
             settle(x_tally.at[:, pl.ds(0, per)], x_recv.at[p, t])
             wide_x = x_img[p, pl.ds(at, per)].reshape(per * rows, chans).astype(F32)
             u = layer_norm(wide_x, g1[...], o1[...]).astype(BF16)
-            for i in range(SWAPS):
-                span = pl.ds(piece * i, piece)
-                before = h_mine[p, span, :] if t else widen(b1_col[pl.ds(piece * i % hid, piece), :], wide)
+            last = t == len(x_parts[p]) - 1
+            blocks = PAIR if last else 1
+            height = PAIR * hid // blocks
+            for i in range(blocks):
+                span = pl.ds(height * i, height)
+                before = h_mine[p, span, :] if t else widen(jnp.concatenate([b1_col[...]] * (height // hid), axis=0), wide)
                 h_mine[p, span, :] = before + jnp.dot(w1_t[span, pl.ds(at * rows, per * rows)], u, preferred_element_type=F32)
-                if t == len(x_parts[p]) - 1:
-                    remote(h_mine.at[p, span, :], h_other.at[p, span, :], h_send.at[p, i], h_recv.at[p, i], other)
+                for s in range(SWAPS // blocks * i, SWAPS // blocks * (i + 1)) if last else ():
+                    swap = pl.ds(piece * s, piece)
+                    remote(h_mine.at[p, swap, :], h_other.at[p, swap, :], h_send.at[p, s], h_recv.at[p, s], other)
             at += per
 
     def activate(p):
@@ -231,7 +228,7 @@
         b2_col[pl.ds(rows * s, rows), :] = jnp.broadcast_to(tail[:, s : s + 1], (rows, LANES))
 
     half_sum(0)
-    settle(far, w_recv.at[1, 1])
+    settle(w_tally, w_recv.at[1])
     for q in range(pairs):
         w2_big[pl.ds(2 * rows * q, 2 * rows), :] = jnp.concatenate(expand(w2_all, q), axis=0).astype(BF16)
     for c in chan_loads:
@@ -331,7 +328,7 @@
                 sem((5,)),
                 sem((8,)),
                 sem((2, sum(len(parts) for parts in z_parts))),
-                sem((2,)), sem((2, 2)),
+                sem((2,)), sem((2,)),
                 sem, sem,
                 sem((PAIR,)), sem((PAIR, max(len(parts) for parts in x_parts))),
                 sem((PAIR, SWAPS)), sem((PAIR, SWAPS)),

time: 45 us -> 47.2 us (1.049); the launches traced: 44.8 us -> 46.4 us
  Pallas kernels: 43.8 us -> 45.4 us
    pallas_call x1, Pallas kernels: 43.8 us -> 45.4 us  [local_layer(): pl.pallas_call(functools.partial(mixer_kernel, n, x_parts, z_parts, b_aft...]
where the time goes in v7:
time: 47.2 us; the launch traced here: 46.4 us
  Pallas kernels  45.4 us (96%)
  local copies, waits for them, and re-layouts  1.02 us (2%)
    pallas_call x1, Pallas kernels, local_layer(): pl.pallas_call(functools.partial(mixer_kernel, n, x_parts, z_parts, b_aft...  45.4 us
    unnamed x1, local copies, waits for them, and re-layouts  1.02 us

profile of v7, /device:TPU:97, one launch (start us, length us, event | category | flops | bytes accessed | tf_op | source)
XLA Modules:
  0.0 46.4 jit_solution(2977567353717780902)
XLA Ops:
  0.0 45.4 %mixer.1 = (bf16[18,64,512]{2,1,0:T(8,128)(2,1)S(1)}, bf16[2,18,2,512]{3,2,1,0:T(2,128)(2,1)}) custom-call(bf16[18,64,512]{2,1,0:T(8,128)(2,1)} %bitcast.12, bf16[18,256]{1,0:T(8,128)(2,1)} %w1_hbm.1, bf16[18,256]{1,0:T(8,128)(2,1)} %bitcast.13, f32[1,8]{1,0:T(1,128)} %bitcast.20, f32[1,18]{1,0:T(1,128)} %bitcast.21, bf16[512,2048]{1,0:T(8,128)(2,1)} %wc1_hbm.1, ...), custom_call_target="tpu_custom_call" | custom-call | tf_op jit(solution)/shard_map/mixer/pallas_call | solution.py:295
  45.4 1.0 %copy.15 = bf16[64,18,512]{2,0,1:T(8,128)(2,1)} copy(bf16[64,18,512]{2,0,1:T(8,128)(2,1)S(1)} %bitcast.11) | data formatting | bytes 2359296

commit v8 on v7

--- a/solution.py
+++ b/solution.py
@@ -67,6 +67,8 @@
     cols = [lax.rem(my_x + d, side) for d in range(side)]
     lines = [lax.rem(my_y + d, side) * side for d in range(side)]
     chips = [lines[dy] + cols[dx] for dx, dy in send_order(side)]
+    row_chips = [lines[0] + cols[dx] for dx, dy in send_order(side) if dy == 0]
+    col_chips = [lines[dy] + cols[0] for dx, dy in send_order(side) if dx == 0]
     other = me + 1 - 2 * my_core
     n_chips = n // CORES
     _, patches, rows, chans = x_img.shape
@@ -88,8 +90,8 @@
     def remote(src, dst, ss, rs, j):
         pltpu.make_async_remote_copy(src_ref=src, dst_ref=dst, send_sem=ss, recv_sem=rs, device_id={AXIS: j}).start()
 
-    def to_twins(src, dst, ss, rs):
-        for k in chips:
+    def to_twins(src, dst, ss, rs, targets=chips):
+        for k in targets:
             remote(src(k), dst, ss, rs, CORES * k + my_core)
 
     b_all[...] = jnp.zeros_like(b_all)
@@ -128,17 +130,39 @@
         part = pl.ds(sum(x_parts[p][:t]), x_parts[p][t])
         to_twins(lambda k: x_own.at[part, image_rows(k, p), :], x_img.at[p, part, two(my_chip), :], x_send.at[p], x_recv.at[p, t])
 
-    to_twins(lambda k: w1_own, w1_all.at[:, two(my_chip), :], w_send.at[0], w_recv.at[0])
+    halves = (pl.ds(0, (pairs + 1) // 2), pl.ds((pairs + 1) // 2, pairs // 2))
+
+    def first_stage(w, w_own, w_all):
+        for h, near in enumerate((row_chips, col_chips)):
+            to_twins(lambda k: w_own.at[halves[h]], w_all.at[halves[h], two(my_chip), :], w_send.at[w], w_recv.at[w, h, 0], near)
+
+    def second_stage(w, w_all):
+        line = w_all.at[halves[0], pl.ds(pl.multiple_of(2 * side * my_y, 2 * side), 2 * side), :]
+        settle(w_tally.at[pl.ds(0, side - 1), halves[0]], w_recv.at[w, 0, 0])
+        to_twins(lambda k: line, line, w_send.at[w], w_recv.at[w, 0, 1], col_chips)
+        settle(w_tally.at[pl.ds(0, side - 1), halves[1]], w_recv.at[w, 1, 0])
+        for c in [my_chip] + col_chips:
+            block = w_all.at[halves[1], two(c), :]
+            to_twins(lambda k: block, block, w_send.at[w], w_recv.at[w, 1, 1], row_chips)
+
+    def landed(w):
+        for h in range(2):
+            settle(w_tally.at[pl.ds(0, side * (side - 1)), halves[h]], w_recv.at[w, h, 1])
+
+    first_stage(0, w1_own, w1_all)
+    for c in late_weights:
+        c.wait()
+    first_stage(1, w2_own, w2_all)
     to_twins(lambda k: b_own, b_all.at[:, two(my_chip), :], b_send, b_recv)
-    for t in range(len(x_parts[0])):
+    send_x(0, 0)
+    for c in mine + x_mine + smalls:
+        c.wait()
+    second_stage(0, w1_all)
+    for t in range(1, len(x_parts[0])):
         send_x(0, t)
-    for c in late_weights:
-        c.wait()
-    to_twins(lambda k: w2_own, w2_all.at[:, two(my_chip), :], w_send.at[1], w_recv.at[1])
+    second_stage(1, w2_all)
     for t in range(len(x_parts[1])):
         send_x(1, t)
-    for c in mine + x_mine + smalls:
-        c.wait()
 
     even = lax.rem(lax.broadcasted_iota(jnp.int32, (rows, hid), 0), 2) == 0
     keep = (lax.rem(lax.broadcasted_iota(jnp.int32, (rows, 2 * hid), 0), 2) == 0) == (
@@ -151,7 +175,7 @@
         second = jnp.where(even, pltpu.roll(wq, rows - 1, 0), wq)
         return [jnp.where(keep, jnp.concatenate([d, d], axis=1), 0.0) for d in (first, second)]
 
-    settle(w_tally, w_recv.at[0])
+    landed(0)
     q = 0
     while q < pairs:
         group = [q] if q + 1 == pairs else [q, q + 1]
@@ -228,7 +252,7 @@
         b2_col[pl.ds(rows * s, rows), :] = jnp.broadcast_to(tail[:, s : s + 1], (rows, LANES))
 
     half_sum(0)
-    settle(w_tally, w_recv.at[1])
+    landed(1)
     for q in range(pairs):
         w2_big[pl.ds(2 * rows * q, 2 * rows), :] = jnp.concatenate(expand(w2_all, q), axis=0).astype(BF16)
     for c in chan_loads:
@@ -328,7 +352,7 @@
                 sem((5,)),
                 sem((8,)),
                 sem((2, sum(len(parts) for parts in z_parts))),
-                sem((2,)), sem((2,)),
+                sem((2,)), sem((2, 2, 2)),
                 sem, sem,
                 sem((PAIR,)), sem((PAIR, max(len(parts) for parts in x_parts))),
                 sem((PAIR, SWAPS)), sem((PAIR, SWAPS)),

time: 47.2 us -> 45.7 us (0.968); the launches traced: 46.4 us -> 45.5 us
  Pallas kernels: 45.4 us -> 44.5 us
    pallas_call x1, Pallas kernels: 45.4 us -> 44.5 us  [local_layer(): pl.pallas_call(functools.partial(mixer_kernel, n, x_parts, z_parts, b_aft...]
where the time goes in v8:
time: 45.7 us; the launch traced here: 45.5 us
  Pallas kernels  44.5 us (97%)
  local copies, waits for them, and re-layouts  1.02 us (2%)
    pallas_call x1, Pallas kernels, local_layer(): pl.pallas_call(functools.partial(mixer_kernel, n, x_parts, z_parts, b_aft...  44.5 us
    unnamed x1, local copies, waits for them, and re-layouts  1.02 us

profile of v8, /device:TPU:97, one launch (start us, length us, event | category | flops | bytes accessed | tf_op | source)
XLA Modules:
  0.0 45.5 jit_solution(18112539477680972977)
XLA Ops:
  0.0 44.5 %mixer.1 = (bf16[18,64,512]{2,1,0:T(8,128)(2,1)S(1)}, bf16[2,18,2,512]{3,2,1,0:T(2,128)(2,1)}) custom-call(bf16[18,64,512]{2,1,0:T(8,128)(2,1)} %bitcast.12, bf16[18,256]{1,0:T(8,128)(2,1)} %w1_hbm.1, bf16[18,256]{1,0:T(8,128)(2,1)} %bitcast.13, f32[1,8]{1,0:T(1,128)} %bitcast.20, f32[1,18]{1,0:T(1,128)} %bitcast.21, bf16[512,2048]{1,0:T(8,128)(2,1)} %wc1_hbm.1, ...), custom_call_target="tpu_custom_call" | custom-call | tf_op jit(solution)/shard_map/mixer/pallas_call | solution.py:319
  44.5 1.0 %copy.15 = bf16[64,18,512]{2,0,1:T(8,128)(2,1)} copy(bf16[64,18,512]{2,0,1:T(8,128)(2,1)S(1)} %bitcast.11) | data formatting | bytes 2359296

commit v9 on v6

--- a/solution.py
+++ b/solution.py
@@ -27,7 +27,9 @@
 
 
 def gelu(a):
-    return 0.5 * a * (1.0 + jnp.tanh(math.sqrt(2.0 / math.pi) * (a + 0.044715 * (a * a * a))))
+    scale = math.sqrt(2.0 / math.pi)
+    half = 0.5 * a
+    return half + half * jnp.tanh(a * (scale + (scale * 0.044715) * (a * a)))
 
 
 def widen(column, copies):
@@ -172,12 +174,16 @@
             settle(x_tally.at[:, pl.ds(0, per)], x_recv.at[p, t])
             wide_x = x_img[p, pl.ds(at, per)].reshape(per * rows, chans).astype(F32)
             u = layer_norm(wide_x, g1[...], o1[...]).astype(BF16)
-            for i in range(SWAPS):
-                span = pl.ds(piece * i, piece)
-                before = h_mine[p, span, :] if t else widen(b1_col[pl.ds(piece * i % hid, piece), :], wide)
+            last = t == len(x_parts[p]) - 1
+            blocks = PAIR if last else 1
+            height = PAIR * hid // blocks
+            for i in range(blocks):
+                span = pl.ds(height * i, height)
+                before = h_mine[p, span, :] if t else widen(jnp.concatenate([b1_col[...]] * (height // hid), axis=0), wide)
                 h_mine[p, span, :] = before + jnp.dot(w1_t[span, pl.ds(at * rows, per * rows)], u, preferred_element_type=F32)
-                if t == len(x_parts[p]) - 1:
-                    remote(h_mine.at[p, span, :], h_other.at[p, span, :], h_send.at[p, i], h_recv.at[p, i], other)
+                for s in range(SWAPS // blocks * i, SWAPS // blocks * (i + 1)) if last else ():
+                    swap = pl.ds(piece * s, piece)
+                    remote(h_mine.at[p, swap, :], h_other.at[p, swap, :], h_send.at[p, s], h_recv.at[p, s], other)
             at += per
 
     def activate(p):

time: 45 us -> 44.8 us (level)
  no operation moved by 1% of the time
where the time goes in v9:
time: 44.8 us; the launch traced here: 44.6 us
  Pallas kernels  43.6 us (97%)
  local copies, waits for them, and re-layouts  1.02 us (2%)
    pallas_call x1, Pallas kernels, local_layer(): pl.pallas_call(functools.partial(mixer_kernel, n, x_parts, z_parts, b_aft...  43.6 us
    unnamed x1, local copies, waits for them, and re-layouts  1.02 us

profile of v9, /device:TPU:97, one launch (start us, length us, event | category | flops | bytes accessed | tf_op | source)
XLA Modules:
  0.0 44.6 jit_solution(4731815494029411950)
XLA Ops:
  0.0 43.6 %mixer.1 = (bf16[18,64,512]{2,1,0:T(8,128)(2,1)S(1)}, bf16[2,18,2,512]{3,2,1,0:T(2,128)(2,1)}) custom-call(bf16[18,64,512]{2,1,0:T(8,128)(2,1)} %bitcast.12, bf16[18,256]{1,0:T(8,128)(2,1)} %w1_hbm.1, bf16[18,256]{1,0:T(8,128)(2,1)} %bitcast.13, f32[1,8]{1,0:T(1,128)} %bitcast.20, f32[1,18]{1,0:T(1,128)} %bitcast.21, bf16[512,2048]{1,0:T(8,128)(2,1)} %wc1_hbm.1, ...), custom_call_target="tpu_custom_call" | custom-call | tf_op jit(solution)/shard_map/mixer/pallas_call | solution.py:304
  43.6 1.0 %copy.15 = bf16[64,18,512]{2,0,1:T(8,128)(2,1)} copy(bf16[64,18,512]{2,0,1:T(8,128)(2,1)S(1)} %bitcast.11) | data formatting | bytes 2359296

commit v10 on v9

--- a/solution.py
+++ b/solution.py
@@ -283,7 +283,7 @@
     settle(b_tally, b_send)
 
 
-def solution(mesh, x_split=((4, 3, 2), (1,)), z_split=((2, 1), (4, 3, 2)), b_after=0, ff_tile=512):
+def solution(mesh, x_split=((4, 3, 2), (1,)), z_split=((2, 1), (1, 1, 1)), b_after=0, ff_tile=512):
     row_spec = P("dp", AXIS, None)
     n = mesh.shape[AXIS]
 

time: 44.8 us -> 45.1 us (level)
  no operation moved by 1% of the time
where the time goes in v10:
time: 45.1 us; the launch traced here: 44.9 us
  Pallas kernels  43.9 us (97%)
  local copies, waits for them, and re-layouts  1.02 us (2%)
    pallas_call x1, Pallas kernels, local_layer(): pl.pallas_call(functools.partial(mixer_kernel, n, x_parts, z_parts, b_aft...  43.9 us
    unnamed x1, local copies, waits for them, and re-layouts  1.02 us

profile of v10, /device:TPU:97, one launch (start us, length us, event | category | flops | bytes accessed | tf_op | source)
XLA Modules:
  0.0 44.9 jit_solution(16577380568530589238)
XLA Ops:
  0.0 43.9 %mixer.1 = (bf16[18,64,512]{2,1,0:T(8,128)(2,1)S(1)}, bf16[2,18,2,512]{3,2,1,0:T(2,128)(2,1)}) custom-call(bf16[18,64,512]{2,1,0:T(8,128)(2,1)} %bitcast.12, bf16[18,256]{1,0:T(8,128)(2,1)} %w1_hbm.1, bf16[18,256]{1,0:T(8,128)(2,1)} %bitcast.13, f32[1,8]{1,0:T(1,128)} %bitcast.20, f32[1,18]{1,0:T(1,128)} %bitcast.21, bf16[512,2048]{1,0:T(8,128)(2,1)} %wc1_hbm.1, ...), custom_call_target="tpu_custom_call" | custom-call | tf_op jit(solution)/shard_map/mixer/pallas_call | solution.py:304
  43.9 1.0 %copy.15 = bf16[64,18,512]{2,0,1:T(8,128)(2,1)} copy(bf16[64,18,512]{2,0,1:T(8,128)(2,1)S(1)} %bitcast.11) | data formatting | bytes 2359296

commit v11 on v10

--- a/solution.py
+++ b/solution.py
@@ -283,7 +283,7 @@
     settle(b_tally, b_send)
 
 
-def solution(mesh, x_split=((4, 3, 2), (1,)), z_split=((2, 1), (1, 1, 1)), b_after=0, ff_tile=512):
+def solution(mesh, x_split=((4, 3, 2), (1,)), z_split=((2, 1), (3, 2, 1)), b_after=0, ff_tile=512):
     row_spec = P("dp", AXIS, None)
     n = mesh.shape[AXIS]
 

time: 45.1 us -> 45.9 us (1.018)
  Pallas kernels: 43.9 us -> 44.7 us
    pallas_call x1, Pallas kernels: 43.9 us -> 44.7 us  [local_layer(): pl.pallas_call(functools.partial(mixer_kernel, n, x_parts, z_parts, b_aft...]
where the time goes in v11:
time: 45.9 us; the launch traced here: 45.7 us
  Pallas kernels  44.7 us (97%)
  local copies, waits for them, and re-layouts  1.02 us (2%)
    pallas_call x1, Pallas kernels, local_layer(): pl.pallas_call(functools.partial(mixer_kernel, n, x_parts, z_parts, b_aft...  44.7 us
    unnamed x1, local copies, waits for them, and re-layouts  1.02 us

profile of v11, /device:TPU:97, one launch (start us, length us, event | category | flops | bytes accessed | tf_op | source)
XLA Modules:
  0.0 45.7 jit_solution(11384068199762052258)
XLA Ops:
  0.0 44.7 %mixer.1 = (bf16[18,64,512]{2,1,0:T(8,128)(2,1)S(1)}, bf16[2,18,2,512]{3,2,1,0:T(2,128)(2,1)}) custom-call(bf16[18,64,512]{2,1,0:T(8,128)(2,1)} %bitcast.12, bf16[18,256]{1,0:T(8,128)(2,1)} %w1_hbm.1, bf16[18,256]{1,0:T(8,128)(2,1)} %bitcast.13, f32[1,8]{1,0:T(1,128)} %bitcast.20, f32[1,18]{1,0:T(1,128)} %bitcast.21, bf16[512,2048]{1,0:T(8,128)(2,1)} %wc1_hbm.1, ...), custom_call_target="tpu_custom_call" | custom-call | tf_op jit(solution)/shard_map/mixer/pallas_call | solution.py:304
  44.7 1.0 %copy.15 = bf16[64,18,512]{2,0,1:T(8,128)(2,1)} copy(bf16[64,18,512]{2,0,1:T(8,128)(2,1)S(1)} %bitcast.11) | data formatting | bytes 2359296

commit v12 on v9

--- a/solution.py
+++ b/solution.py
@@ -252,10 +252,8 @@
         part = pl.ds(at, per)
         expand_channels(slot, per)
         following = steps[i + 1] if i + 1 < len(steps) else None
-        if following and i:
-            if following[0] != p:
-                g = activate(following[0])
-            prepare(1 - slot, following[0], g, *following[1:])
+        if following and i and following[0] == p:
+            prepare(1 - slot, p, g, *following[1:])
         contract_channels(slot, p, at, per)
         if own:
             own[-1][0].wait()
@@ -265,6 +263,9 @@
         to_twins(lambda k: z_img.at[p, part, two(k), :], out_ref.at[part, image_rows(my_chip, p), :], z_send.at[p], z_recv.at[p])
         if i == 0:
             prepare(1 - slot, p, g, *following[1:])
+        elif following and following[0] != p:
+            g = activate(following[0])
+            prepare(1 - slot, following[0], g, *following[1:])
         if i == b_after:
             half_sum(1)
 

time: 44.8 us -> 45 us (level)
  no operation moved by 1% of the time
where the time goes in v12:
time: 45 us; the launch traced here: 44.8 us
  Pallas kernels  43.8 us (97%)
  local copies, waits for them, and re-layouts  1.02 us (2%)
    pallas_call x1, Pallas kernels, local_layer(): pl.pallas_call(functools.partial(mixer_kernel, n, x_parts, z_parts, b_aft...  43.8 us
    unnamed x1, local copies, waits for them, and re-layouts  1.02 us

profile of v12, /device:TPU:97, one launch (start us, length us, event | category | flops | bytes accessed | tf_op | source)
XLA Modules:
  0.0 44.8 jit_solution(15522429700846627823)
XLA Ops:
  0.0 43.8 %mixer.1 = (bf16[18,64,512]{2,1,0:T(8,128)(2,1)S(1)}, bf16[2,18,2,512]{3,2,1,0:T(2,128)(2,1)}) custom-call(bf16[18,64,512]{2,1,0:T(8,128)(2,1)} %bitcast.12, bf16[18,256]{1,0:T(8,128)(2,1)} %w1_hbm.1, bf16[18,256]{1,0:T(8,128)(2,1)} %bitcast.13, f32[1,8]{1,0:T(1,128)} %bitcast.20, f32[1,18]{1,0:T(1,128)} %bitcast.21, bf16[512,2048]{1,0:T(8,128)(2,1)} %wc1_hbm.1, ...), custom_call_target="tpu_custom_call" | custom-call | tf_op jit(solution)/shard_map/mixer/pallas_call | solution.py:305
  43.8 1.0 %copy.15 = bf16[64,18,512]{2,0,1:T(8,128)(2,1)} copy(bf16[64,18,512]{2,0,1:T(8,128)(2,1)S(1)} %bitcast.11) | data formatting | bytes 2359296
